TPU v7x, 16 devices: a 4x2x1 block of a 4x4x8 slice. The times are simulated.
16 devices in a mesh: dp: 2 (over y, z), ep: 8 (over x, core).
Axes of the slice: x: 4, y: 2, z: 1, core: 2. Of those that a mesh axis runs over, the one named last changes fastest.
The devices are a block of a 4x4x8 slice.
Arguments:
- tokens: bfloat16 [2, 32, 512, 1536], P(None, ('dp', 'ep')), parts along dimension 1
- expert_ids: int32 [2, 16384, 6], P(None, ('dp', 'ep')), parts along dimension 1
- route_weights: float32 [2, 16384, 6], P(None, ('dp', 'ep')), parts along dimension 1
- attn_norm: bfloat16 [1536], replicated
- w_query: bfloat16 [1536, 12, 128], replicated
- w_key: bfloat16 [1536, 12, 128], replicated
- w_value: bfloat16 [1536, 12, 128], replicated
- w_out: bfloat16 [12, 128, 1536], replicated
- ffn_norm: bfloat16 [1536], replicated
- w_gate: bfloat16 [64, 1536, 512], P('ep')
- w_up: bfloat16 [64, 1536, 512], P('ep')
- w_down: bfloat16 [64, 512, 1536], P('ep')
- shared_gate: bfloat16 [1536, 1024], replicated
- shared_up: bfloat16 [1536, 1024], replicated
- shared_down: bfloat16 [1024, 1536], replicated
Outputs:
- output: bfloat16 [2, 32, 512, 1536], P(None, ('dp', 'ep')), parts along dimension 1
There are 2 independent parts. A program takes and returns all parts, laid end to end along the dimension named above; an argument that names none is the same for every part.
All inputs are finite; a program needn't handle non-finite values.
Results may differ from a plain program's by a relative error of at most 0.00977925.
Values are sent between devices in bfloat16 or wider.
A program may use at most 768 MiB of HBM per device.

v0:
```python
import jax
import jax.numpy as jnp
from jax import lax
from jax.sharding import PartitionSpec as P

NORM_EPS = 1e-6
CAP_FACTOR = 2
SLOT_ALIGN = 8


def capacity_of(n_tok, top_count, experts):
    return SLOT_ALIGN * ((CAP_FACTOR * n_tok * top_count + SLOT_ALIGN * experts - 1) // (SLOT_ALIGN * experts))


def rms_norm(in_vals, norm_gain):
    wide_vals = in_vals.astype(jnp.float32)
    inv_rms = lax.rsqrt(jnp.mean(wide_vals * wide_vals, axis=-1, keepdims=True) + NORM_EPS)
    return (wide_vals * inv_rms * norm_gain.astype(jnp.float32)).astype(jnp.bfloat16)


def attention_block(seq_rows, attn_norm, w_query, w_key, w_value, w_out):
    normed = rms_norm(seq_rows, attn_norm)
    queries = jnp.einsum("...sd,dhe->...she", normed, w_query, preferred_element_type=jnp.float32).astype(jnp.bfloat16)
    key_rows = jnp.einsum("...sd,dhe->...she", normed, w_key, preferred_element_type=jnp.float32).astype(jnp.bfloat16)
    value_rows = jnp.einsum("...sd,dhe->...she", normed, w_value, preferred_element_type=jnp.float32).astype(jnp.bfloat16)
    seq_len = seq_rows.shape[-2]
    scores = jnp.einsum("...qhe,...khe->...hqk", queries, key_rows, preferred_element_type=jnp.float32) * (w_query.shape[-1] ** -0.5)
    causal = jnp.arange(seq_len)[:, None] >= jnp.arange(seq_len)[None, :]
    attn_probs = jax.nn.softmax(jnp.where(causal, scores, -jnp.inf), axis=-1).astype(jnp.bfloat16)
    head_mix = jnp.einsum("...hqk,...khe->...qhe", attn_probs, value_rows, preferred_element_type=jnp.float32).astype(jnp.bfloat16)
    attn_out = jnp.einsum("...qhe,hed->...qd", head_mix, w_out, preferred_element_type=jnp.float32)
    return (seq_rows.astype(jnp.float32) + attn_out).astype(jnp.bfloat16)


def swiglu(in_rows, gate_w, up_w, down_w):
    gate_act = jnp.dot(in_rows, gate_w, preferred_element_type=jnp.float32)
    up_act = jnp.dot(in_rows, up_w, preferred_element_type=jnp.float32)
    hidden = (jax.nn.silu(gate_act) * up_act).astype(jnp.bfloat16)
    return jnp.dot(hidden, down_w, preferred_element_type=jnp.float32).astype(jnp.bfloat16)


def route_plan(flat_ids, experts, slot_cap):
    n_rows = flat_ids.shape[0]
    sort_order = jnp.argsort(flat_ids, stable=True).astype(jnp.int32)
    counts = jnp.bincount(flat_ids, length=experts)
    starts = jnp.cumsum(counts) - counts
    sorted_rank = jnp.zeros((n_rows,), jnp.int32).at[sort_order].set(jnp.arange(n_rows, dtype=jnp.int32))
    slot_ids = sorted_rank - starts[flat_ids]
    src_pos = sort_order[jnp.minimum(starts[:, None] + jnp.arange(slot_cap)[None, :], n_rows - 1)]
    return slot_ids, src_pos


def solution(mesh):
    group_size = mesh.shape["ep"]

    def device_step(tokens, expert_ids, route_weights, attn_norm, w_query, w_key, w_value, w_out, ffn_norm, w_gate, w_up, w_down, shared_gate, shared_up, shared_down):
        n_micro, n_seq, seq_len, d_model = tokens.shape
        n_tok = n_seq * seq_len
        top_count = expert_ids.shape[-1]
        local_experts = w_gate.shape[0]
        experts = local_experts * group_size
        slot_cap = capacity_of(n_tok, top_count, experts)
        micro_outs = []
        for micro_idx in range(n_micro):
            residual = attention_block(tokens[micro_idx], attn_norm, w_query, w_key, w_value, w_out).reshape(n_tok, d_model)
            normed = rms_norm(residual, ffn_norm)
            shared_out = swiglu(normed, shared_gate, shared_up, shared_down)
            flat_ids = expert_ids[micro_idx].reshape(-1)
            slot_ids, src_pos = route_plan(flat_ids, experts, slot_cap)
            send_rows = jnp.take(normed, src_pos // top_count, axis=0)
            recv_rows = lax.all_to_all(send_rows, "ep", 0, 0, tiled=True)
            recv_rows = recv_rows.reshape(group_size, local_experts, slot_cap, d_model)
            gate_act = jnp.einsum("secd,edf->secf", recv_rows, w_gate, preferred_element_type=jnp.float32)
            up_act = jnp.einsum("secd,edf->secf", recv_rows, w_up, preferred_element_type=jnp.float32)
            hidden = (jax.nn.silu(gate_act) * up_act).astype(jnp.bfloat16)
            expert_out = jnp.einsum("secf,efd->secd", hidden, w_down, preferred_element_type=jnp.float32).astype(jnp.bfloat16)
            back_rows = lax.all_to_all(expert_out.reshape(experts, slot_cap, d_model), "ep", 0, 0, tiled=True)
            picked = jnp.take(back_rows.reshape(experts * slot_cap, d_model), flat_ids * slot_cap + slot_ids, axis=0)
            picked = picked.reshape(n_tok, top_count, d_model)
            routed = jnp.sum(picked.astype(jnp.float32) * route_weights[micro_idx][:, :, None], axis=1)
            layer_rows = residual.astype(jnp.float32) + shared_out.astype(jnp.float32) + routed
            micro_outs.append(layer_rows.astype(jnp.bfloat16).reshape(n_seq, seq_len, d_model))
        return jnp.stack(micro_outs)

    token_spec = P(None, ("dp", "ep"), None, None)
    route_spec = P(None, ("dp", "ep"), None)
    rep_spec = P()
    expert_spec = P("ep", None, None)
    in_specs = (token_spec, route_spec, route_spec, rep_spec, rep_spec, rep_spec, rep_spec, rep_spec, rep_spec, expert_spec, expert_spec, expert_spec, rep_spec, rep_spec, rep_spec)
    return jax.shard_map(device_step, mesh=mesh, in_specs=in_specs, out_specs=token_spec, check_vma=False)
```

profile of v0, /device:TPU:112, one launch (start us, length us, event | category | flops | bytes accessed | tf_op | source)
XLA Modules:
  0.0 2424.7 jit_solution(10727584641786578356)
XLA Ops:
  5.6 42.9 %scatter_custom_fusion = s32[64]{0:T(128)S(1)} fusion(s32[6144]{0:T(1024)S(1)} %bitcast.381, s32[6144]{0:T(1024)S(1)} %broadcast.518, s32[]{:T(128)} %constant.45.clone.1), kind=kCustom, calls=%fused_computation.306 | custom fusion | flops 6144 | bytes 260 | tf_op jit(solution)/shard_map/scatter-add | solution.py:45
  57.8 68.2 %gather_fusion = s32[12288]{0:T(1024)S(1)} fusion(s32[6144]{0:T(1024)S(1)} %get-tuple-element.9, s32[12288]{0:T(1024)S(1)} %broadcast_clamp_fusion.3), kind=kCustom, calls=%fused_computation.4 | custom fusion | bytes 147456 | tf_op jit(solution)/shard_map/gather | solution.py:49
  181.1 29.4 %fusion.163 = (f32[2,12,512]{2,1,0:T(8,128)}, f32[2,12,512,512]{2,3,1,0:T(8,128)}) fusion(f32[2,12,512,512]{2,3,1,0:T(8,128)} %fusion.97, pred[512,512]{0,1:T(8,128)(4,1)S(1)} %iota_compare_fusion), kind=kOutput, calls=%fused_computation.325 | output fusion | flops 37749248 | bytes 50642944 | tf_op jit(solution)/shard_map/sub | solution.py:29
  210.5 28.5 %fusion.162 = (f32[2,12,512]{2,1,0:T(8,128)S(1)}, f32[2,12,512,512]{2,3,1,0:T(8,128)}) fusion(f32[2,12,512,512]{2,3,1,0:T(8,128)} %fusion.106, pred[512,512]{0,1:T(8,128)(4,1)S(1)} %iota_compare_fusion), kind=kOutput, calls=%fused_computation.324 | output fusion | flops 37749248 | bytes 50642944 | tf_op jit(solution)/shard_map/sub | solution.py:29
  298.6 75.6 %gather_fusion.2 = bf16[12288,1536]{1,0:T(8,128)(2,1)} fusion(bf16[1024,1536]{1,0:T(8,128)(2,1)} %get-tuple-element.143, s32[12288]{0:T(1024)S(1)} %broadcast_clamp_fusion.1), kind=kCustom, calls=%fused_computation.clone | custom fusion | bytes 75546624 | tf_op jit(solution)/shard_map/jit(_take)/gather | solution.py:70
  412.1 43.1 %scatter_custom_fusion.2 = s32[64]{0:T(128)S(1)} fusion(s32[6144]{0:T(1024)S(1)} %bitcast.382, s32[6144]{0:T(1024)} %copy-done.23, s32[]{:T(128)} %constant.45.clone.1), kind=kCustom, calls=%fused_computation.304 | custom fusion | flops 6144 | bytes 768 | tf_op jit(solution)/shard_map/scatter-add | solution.py:45
  463.1 68.0 %gather_fusion.1 = s32[12288]{0:T(1024)S(1)} fusion(s32[6144]{0:T(1024)S(1)} %get-tuple-element.10, s32[12288]{0:T(1024)S(1)} %broadcast_clamp_fusion.2), kind=kCustom, calls=%fused_computation.5 | custom fusion | bytes 147456 | tf_op jit(solution)/shard_map/gather | solution.py:49
  531.5 75.7 %gather_fusion.4 = bf16[12288,1536]{1,0:T(8,128)(2,1)} fusion(bf16[1024,1536]{1,0:T(8,128)(2,1)} %get-tuple-element.144, s32[12288]{0:T(1024)S(1)} %broadcast_clamp_fusion), kind=kCustom, calls=%fused_computation.2.clone | custom fusion | bytes 75546624 | tf_op jit(solution)/shard_map/jit(_take)/gather | solution.py:70
  633.2 184.3 %all-to-all-done = bf16[64,192,1536]{2,1,0:T(8,128)(2,1)} async-done(((bf16[64,192,1536]{2,1,0:T(8,128)(2,1)}), bf16[64,192,1536]{2,1,0:T(8,128)(2,1)}, u32[]{:S(2)}, u32[]{:S(2)}) %all-to-all-start) | async-done | bytes 37748768 | tf_op jit(solution)/shard_map/all_to_all | solution.py:71
  825.4 31.3 %fusion.6 = f32[8,8,192,512]{3,2,1,0:T(8,128)} fusion(bf16[8,8,192,1536]{3,2,1,0:T(8,128)(2,1)} %bitcast.81, bf16[8,1536,512]{2,1,0:T(8,128)(2,1)} %param.29), kind=kOutput, calls=%fused_computation.22 | convolution fusion | flops 19327352832 | bytes 75497472 | tf_op jit(solution)/shard_map/secd,edf->secf/dot_general | solution.py:74
  856.7 57.6 %convert_bitcast_fusion.1 = bf16[8,8,192,1536]{3,2,0,1:T(8,128)(2,1)} fusion(f32[8,8,192,512]{3,2,1,0:T(8,128)} %fusion.6, bf16[8,512,1536]{2,1,0:T(8,128)(2,1)} %param.30, bf16[8,8,192,1536]{3,2,1,0:T(8,128)(2,1)} %bitcast.81, bf16[8,1536,512]{2,1,0:T(8,128)(2,1)} %param.28), kind=kOutput, calls=%fused_computation.15 | convolution fusion | flops 38711328768 | bytes 125829120 | tf_op jit(solution)/shard_map/secf,efd->secd/dot_general | solution.py:76
  940.3 294.2 %all-to-all-done.2 = bf16[64,192,1536]{2,1,0:T(8,128)(2,1)} async-done(((bf16[64,192,1536]{2,1,0:T(8,128)(2,1)}), bf16[64,192,1536]{2,1,0:T(8,128)(2,1)}, u32[]{:S(2)}, u32[]{:S(2)}) %all-to-all-start.2) | async-done | bytes 37748768 | tf_op jit(solution)/shard_map/all_to_all | solution.py:71
  1242.4 31.2 %fusion.2 = f32[8,8,192,512]{3,2,1,0:T(8,128)} fusion(bf16[8,8,192,1536]{3,2,1,0:T(8,128)(2,1)} %bitcast.172, bf16[8,1536,512]{2,1,0:T(8,128)(2,1)} %param.29), kind=kOutput, calls=%fused_computation.18 | convolution fusion | flops 19327352832 | bytes 75497472 | tf_op jit(solution)/shard_map/secd,edf->secf/dot_general | solution.py:74
  1273.6 57.6 %convert_bitcast_fusion = bf16[8,8,192,1536]{3,2,0,1:T(8,128)(2,1)} fusion(f32[8,8,192,512]{3,2,1,0:T(8,128)} %fusion.2, bf16[8,512,1536]{2,1,0:T(8,128)(2,1)} %param.30, bf16[8,8,192,1536]{3,2,1,0:T(8,128)(2,1)} %bitcast.172, bf16[8,1536,512]{2,1,0:T(8,128)(2,1)} %param.28), kind=kOutput, calls=%fused_computation.14 | convolution fusion | flops 38711328768 | bytes 125829120 | tf_op jit(solution)/shard_map/secf,efd->secd/dot_general | solution.py:76
  1357.2 294.2 %all-to-all-done.1 = bf16[64,192,1536]{2,1,0:T(8,128)(2,1)} async-done(((bf16[64,192,1536]{2,1,0:T(8,128)(2,1)}), bf16[64,192,1536]{2,1,0:T(8,128)(2,1)}, u32[]{:S(2)}, u32[]{:S(2)}) %all-to-all-start.1) | async-done | bytes 37748768 | tf_op jit(solution)/shard_map/all_to_all | solution.py:77
  1722.4 35.6 %compare_and_fusion.3 = (pred[6144]{0:T(1024)(128)(4,1)S(1)}, s32[6144]{0:T(1024)S(1)}) fusion(s32[6144]{0:T(1024)S(1)} %scatter_custom_fusion.1, pred[6144]{0:T(1024)(128)(4,1)S(1)} %get-tuple-element.69, pred[6144]{0:T(1024)(128)(4,1)S(1)} %get-tuple-element.68, pred[6144]{0:T(1024)(128)(4,1)S(1)} %get-tuple-element.67, ...), kind=kLoop, calls=%fused_computation.289 | loop fusion | flops 405504 | bytes 454884 | tf_op jit(solution)/shard_map/jit(_take)/and | solution.py:78
  1766.9 36.0 %compare_and_fusion.2 = (pred[6144]{0:T(1024)(128)(4,1)S(1)}, s32[6144]{0:T(1024)S(1)}) fusion(s32[6144]{0:T(1024)S(1)} %scatter_custom_fusion.3, pred[6144]{0:T(1024)(128)(4,1)S(1)} %get-tuple-element.126, pred[6144]{0:T(1024)(128)(4,1)S(1)} %get-tuple-element.125, pred[6144]{0:T(1024)(128)(4,1)S(1)} %get-tuple-element.124, ...), kind=kLoop, calls=%fused_computation.288 | loop fusion | flops 405504 | bytes 454884 | tf_op jit(solution)/shard_map/jit(_take)/and | solution.py:78
  1816.5 131.5 %gather_fusion.3 = bf16[6144,1536]{1,0:T(8,128)(2,1)} fusion(bf16[12288,1536]{1,0:T(8,128)(2,1)} %bitcast.92, s32[6144]{0:T(1024)S(1)} %broadcast_clamp_fusion.5), kind=kCustom, calls=%fused_computation.1.clone | custom fusion | bytes 37773312 | tf_op jit(solution)/shard_map/jit(_take)/gather | solution.py:78
  1968.7 41.8 %reshape.328 = f32[1024,6,1536]{2,1,0:T(8,128)} reshape(f32[6144,1536]{1,0:T(8,128)} %select_convert_fusion.1) | data formatting | bytes 75497472 | tf_op jit(solution)/shard_map/convert_element_type | solution.py:80
  2010.6 57.7 %all-to-all-done.3 = bf16[64,192,1536]{2,1,0:T(8,128)(2,1)} async-done(((bf16[64,192,1536]{2,1,0:T(8,128)(2,1)}), bf16[64,192,1536]{2,1,0:T(8,128)(2,1)}, u32[]{:S(2)}, u32[]{:S(2)}) %all-to-all-start.3) | async-done | bytes 37748768 | tf_op jit(solution)/shard_map/all_to_all | solution.py:77
  2068.2 131.5 %gather_fusion.5 = bf16[6144,1536]{1,0:T(8,128)(2,1)} fusion(bf16[12288,1536]{1,0:T(8,128)(2,1)} %bitcast.180, s32[6144]{0:T(1024)S(1)} %broadcast_clamp_fusion.4), kind=kCustom, calls=%fused_computation.3.clone | custom fusion | bytes 37773312 | tf_op jit(solution)/shard_map/jit(_take)/gather | solution.py:78
  2220.7 41.8 %reshape.331 = f32[1024,6,1536]{2,1,0:T(8,128)} reshape(f32[6144,1536]{1,0:T(8,128)} %select_convert_fusion) | data formatting | bytes 75497472 | tf_op jit(solution)/shard_map/convert_element_type | solution.py:80
  2262.5 64.6 %multiply_reduce_fusion.1 = f32[1024,1536]{1,0:T(8,128)} fusion(f32[1024,6,1536]{2,1,0:T(8,128)} %reshape.328, f32[1024,6]{1,0:T(8,128)} %bitcast.377), kind=kLoop, calls=%fused_computation.13 | loop fusion | flops 17301504 | bytes 44064768 | tf_op jit(solution)/shard_map/reduce_sum | solution.py:80
  2327.1 64.8 %multiply_reduce_fusion = f32[1024,1536]{1,0:T(8,128)} fusion(f32[1024,6,1536]{2,1,0:T(8,128)} %reshape.331, f32[1024,6]{1,0:T(8,128)S(1)} %bitcast.378), kind=kLoop, calls=%fused_computation.12 | loop fusion | flops 17301504 | bytes 44064768 | tf_op jit(solution)/shard_map/reduce_sum | solution.py:80
  (162 shorter events, 436.5 us)
Async XLA Ops:
  0.0 2391.9 %copy-start = (bf16[1024,1536]{1,0:T(8,128)(2,1)S(1)}, bf16[1024,1536]{1,0:T(8,128)(2,1)}, u32[]{:S(2)}) copy-start(bf16[1024,1536]{1,0:T(8,128)(2,1)} %param.33) | copy-start | bytes 9437188
  4.1 44.8 %copy-start.17 = (s32[6144,1]{0,1:T(1,128)}, s32[6144,1]{0,1:T(1,128)S(1)}, u32[]{:S(2)}) copy-start(s32[6144,1]{0,1:T(1,128)S(1)} %reshape_squeeze.11) | copy-start | bytes 73732
  5.5 120.5 %copy-start.13 = (s32[6144]{0:T(1024)}, s32[6144]{0:T(1024)S(1)}, u32[]{:S(2)}) copy-start(s32[6144]{0:T(1024)S(1)} %reshape_squeeze.10) | copy-start | bytes 73732
  5.6 42.9 %copy-start.23 = (s32[6144]{0:T(1024)}, s32[6144]{0:T(1024)S(1)}, u32[]{:S(2)}) copy-start(s32[6144]{0:T(1024)S(1)} %broadcast.518) | copy-start | bytes 73732
  57.8 68.2 %copy-start.1 = (s32[6144]{0:T(1024)}, s32[6144]{0:T(1024)S(1)}, u32[]{:S(2)}) copy-start(s32[6144]{0:T(1024)S(1)} %get-tuple-element.9) | copy-start | bytes 73732
  127.2 13.7 slice-start
  127.2 13.7 slice-start.2
  282.5 10.5 copy-start.19
  282.5 10.6 copy-start.22
  400.3 417.1 %all-to-all-start = ((bf16[64,192,1536]{2,1,0:T(8,128)(2,1)}), bf16[64,192,1536]{2,1,0:T(8,128)(2,1)}, u32[]{:S(2)}, u32[]{:S(2)}) async-start(bf16[64,192,1536]{2,1,0:T(8,128)(2,1)} %broadcast_select_fusion.1), calls=%async_computation | async-start | bytes 75497472 | tf_op jit(solution)/shard_map/all_to_all | solution.py:71
  410.7 44.8 %copy-start.15 = (s32[6144,1]{0,1:T(1,128)}, s32[6144,1]{0,1:T(1,128)S(1)}, u32[]{:S(2)}) copy-start(s32[6144,1]{0,1:T(1,128)S(1)} %reshape_squeeze.13) | copy-start | bytes 73732
  412.1 44.2 %copy-start.11 = (s32[6144]{0:T(1024)}, s32[6144]{0:T(1024)S(1)}, u32[]{:S(2)}) copy-start(s32[6144]{0:T(1024)S(1)} %reshape_squeeze.12) | copy-start | bytes 73732
  463.0 68.1 %copy-start.3 = (s32[6144]{0:T(1024)}, s32[6144]{0:T(1024)S(1)}, u32[]{:S(2)}) copy-start(s32[6144]{0:T(1024)S(1)} %get-tuple-element.10) | copy-start | bytes 73732
  817.5 416.9 %all-to-all-start.2 = ((bf16[64,192,1536]{2,1,0:T(8,128)(2,1)}), bf16[64,192,1536]{2,1,0:T(8,128)(2,1)}, u32[]{:S(2)}, u32[]{:S(2)}) async-start(bf16[64,192,1536]{2,1,0:T(8,128)(2,1)} %broadcast_select_fusion), calls=%async_computation.2 | async-start | bytes 75497472 | tf_op jit(solution)/shard_map/all_to_all | solution.py:71
  1234.4 417.0 %all-to-all-start.1 = ((bf16[64,192,1536]{2,1,0:T(8,128)(2,1)}), bf16[64,192,1536]{2,1,0:T(8,128)(2,1)}, u32[]{:S(2)}, u32[]{:S(2)}) async-start(bf16[64,192,1536]{2,1,0:T(8,128)(2,1)} %bitcast.370), calls=%async_computation.1 | async-start | bytes 75497472 | tf_op jit(solution)/shard_map/all_to_all | solution.py:77
  1651.4 33.1 %copy-start.4 = (s32[6144]{0:T(1024)S(1)}, s32[6144]{0:T(1024)}, u32[]{:S(2)}) copy-start(s32[6144]{0:T(1024)} %copy-done.3) | copy-start | bytes 73732
  1651.4 56.3 %copy-start.7 = (s32[64]{0:T(128)S(1)}, s32[64]{0:T(128)}, u32[]{:S(2)}) copy-start(s32[64]{0:T(128)} %copy-done.6) | copy-start | bytes 772
  1651.4 57.0 %copy-start.9 = (s32[64]{0:T(128)S(1)}, s32[64]{0:T(128)}, u32[]{:S(2)}) copy-start(s32[64]{0:T(128)} %copy-done.8) | copy-start | bytes 772
  1651.4 62.0 %copy-start.18 = (s32[6144,1]{0,1:T(1,128)S(1)}, s32[6144,1]{0,1:T(1,128)}, u32[]{:S(2)}) copy-start(s32[6144,1]{0,1:T(1,128)} %copy-done.17) | copy-start | bytes 73732
  1651.4 70.9 %copy-start.14 = (s32[6144]{0:T(1024)S(1)}, s32[6144]{0:T(1024)}, u32[]{:S(2)}) copy-start(s32[6144]{0:T(1024)} %copy-done.13) | copy-start | bytes 73732
  1651.4 106.6 %copy-start.16 = (s32[6144,1]{0,1:T(1,128)S(1)}, s32[6144,1]{0,1:T(1,128)}, u32[]{:S(2)}) copy-start(s32[6144,1]{0,1:T(1,128)} %copy-done.15) | copy-start | bytes 73732
  1651.5 115.4 %copy-start.12 = (s32[6144]{0:T(1024)S(1)}, s32[6144]{0:T(1024)}, u32[]{:S(2)}) copy-start(s32[6144]{0:T(1024)} %copy-done.11) | copy-start | bytes 73732
  1651.5 416.8 %all-to-all-start.3 = ((bf16[64,192,1536]{2,1,0:T(8,128)(2,1)}), bf16[64,192,1536]{2,1,0:T(8,128)(2,1)}, u32[]{:S(2)}, u32[]{:S(2)}) async-start(bf16[64,192,1536]{2,1,0:T(8,128)(2,1)} %bitcast.369), calls=%async_computation.3 | async-start | bytes 75497472 | tf_op jit(solution)/shard_map/all_to_all | solution.py:77
  2262.5 64.6 %copy-start.10 = (f32[1,1024,6]{2,1,0:T(8,128)S(1)}, f32[1,1024,6]{2,1,0:T(8,128)}, u32[]{:S(2)}) copy-start(f32[1,1024,6]{2,1,0:T(8,128)} %copy.72) | copy-start | bytes 73732
  (11 other events, 79.5 us)
where the time goes:
time: 2440 us; the launch traced here: 2420 us
  waiting for transfers between devices  830 us (34%)
  local copies, waits for them, and re-layouts  752 us (31%)
  other arithmetic  488 us (20%)
  matrix products  321 us (13%)
  starting transfers between devices  31.6 us (1%)
    all_to_all x2, waiting for transfers between devices, device_step(): recv_rows = lax.all_to_all(send_rows, 'ep', 0, 0, tiled=True)  478 us
    all_to_all x2, waiting for transfers between devices, device_step(): lax.all_to_all(expert_out.reshape(experts, slot_cap, d_model), 'ep', 0, 0...  352 us
    gather x2, local copies, waits for them, and re-layouts, device_step(): jnp.take(back_rows.reshape(experts * slot_cap, d_model), flat_ids * slot_...  263 us
    gather x2, local copies, waits for them, and re-layouts, device_step(): send_rows = jnp.take(normed, src_pos // top_count, axis=0)  151 us
    gather x2, local copies, waits for them, and re-layouts, route_plan(): sort_order[jnp.minimum(starts[:, None] + jnp.arange(slot_cap)[None, :], n...  136 us
    reduce_sum x2, other arithmetic, device_step(): jnp.sum(picked.astype(jnp.float32) * route_weights[micro_idx][:, :, None]...  129 us
    dot_general x2, matrix products, device_step(): jnp.einsum('secf,efd->secd', hidden, w_down, preferred_element_type=jnp.f...  115 us
    scatter-add x2, other arithmetic, route_plan(): counts = jnp.bincount(flat_ids, length=experts)  86 us
  transfers between devices with their start and end apart: 4, of which 4 were waited for; matrix products, arithmetic and copies ran while one was open for 33% of the time, Pallas kernels for 0%

commit v1 on v0

v1 whole, which is shorter than its diff:
```python
import functools

import jax
import jax.numpy as jnp
from jax import lax
from jax.experimental import pallas as pl
from jax.experimental.pallas import tpu as pltpu
from jax.sharding import PartitionSpec as P

NORM_EPS = 1e-6
CAP_FACTOR = 2
SLOT_ALIGN = 8
SEG = 16
ROWS = 256
VMEM_LIMIT = 64_000_000


def capacity_of(n_tok, top_count, experts):
    return SLOT_ALIGN * ((CAP_FACTOR * n_tok * top_count + SLOT_ALIGN * experts - 1) // (SLOT_ALIGN * experts))


def rms_norm(in_vals, norm_gain):
    wide_vals = in_vals.astype(jnp.float32)
    inv_rms = lax.rsqrt(jnp.mean(wide_vals * wide_vals, axis=-1, keepdims=True) + NORM_EPS)
    return (wide_vals * inv_rms * norm_gain.astype(jnp.float32)).astype(jnp.bfloat16)


def attention_block(seq_rows, attn_norm, w_query, w_key, w_value, w_out):
    normed = rms_norm(seq_rows, attn_norm)
    queries = jnp.einsum("...sd,dhe->...she", normed, w_query, preferred_element_type=jnp.float32).astype(jnp.bfloat16)
    key_rows = jnp.einsum("...sd,dhe->...she", normed, w_key, preferred_element_type=jnp.float32).astype(jnp.bfloat16)
    value_rows = jnp.einsum("...sd,dhe->...she", normed, w_value, preferred_element_type=jnp.float32).astype(jnp.bfloat16)
    seq_len = seq_rows.shape[-2]
    scores = jnp.einsum("...qhe,...khe->...hqk", queries, key_rows, preferred_element_type=jnp.float32) * (w_query.shape[-1] ** -0.5)
    causal = jnp.arange(seq_len)[:, None] >= jnp.arange(seq_len)[None, :]
    attn_probs = jax.nn.softmax(jnp.where(causal, scores, -jnp.inf), axis=-1).astype(jnp.bfloat16)
    head_mix = jnp.einsum("...hqk,...khe->...qhe", attn_probs, value_rows, preferred_element_type=jnp.float32).astype(jnp.bfloat16)
    attn_out = jnp.einsum("...qhe,hed->...qd", head_mix, w_out, preferred_element_type=jnp.float32)
    return (seq_rows.astype(jnp.float32) + attn_out).astype(jnp.bfloat16)


def swiglu(in_rows, gate_w, up_w, down_w):
    gate_act = jnp.dot(in_rows, gate_w, preferred_element_type=jnp.float32)
    up_act = jnp.dot(in_rows, up_w, preferred_element_type=jnp.float32)
    hidden = (jax.nn.silu(gate_act) * up_act).astype(jnp.bfloat16)
    return jnp.dot(hidden, down_w, preferred_element_type=jnp.float32).astype(jnp.bfloat16)


def route_tables(local_ids, weights, n_local):
    n_src, _, n_tok = local_ids.shape
    hits = local_ids[:, :, None, :] == jnp.arange(n_local)[None, None, :, None]
    mask = jnp.any(hits, axis=1)
    upper = (jnp.arange(n_tok)[:, None] <= jnp.arange(n_tok)[None, :]).astype(jnp.bfloat16)
    running = jnp.dot(mask.astype(jnp.bfloat16).reshape(n_src * n_local, n_tok), upper, preferred_element_type=jnp.float32)
    running = running.astype(jnp.int32).reshape(n_src, n_local, n_tok)
    counts = running[:, :, -1]
    padded = (counts + SEG - 1) // SEG * SEG
    before_e = (jnp.arange(n_local)[:, None] < jnp.arange(n_local)[None, :]).astype(jnp.int32)
    before_s = (jnp.arange(n_src)[:, None] < jnp.arange(n_src)[None, :]).astype(jnp.int32)
    offs = jnp.sum(padded[:, :, None] * before_e[None], axis=1)
    places = jnp.sum(padded[:, None, :] * before_s[:, :, None], axis=0)
    slot_of = offs[:, :, None] + running - 1
    slots = jnp.sum(jnp.where(hits, slot_of[:, None] + 1, 0), axis=2) - 1
    table = jnp.concatenate([offs.reshape(-1), padded.reshape(-1), places.reshape(-1), jnp.sum(padded, axis=0), jnp.sum(padded, axis=1)])
    pad_rows = jnp.full((n_src, 8 - slots.shape[1], n_tok), -1, jnp.int32)
    slot_rows = jnp.concatenate([slots, pad_rows], axis=1)
    cols = jnp.concatenate([slots.astype(jnp.float32), weights], axis=1).transpose(0, 2, 1)
    return table, slot_rows, cols


def gather_kernel(n_src, n_local, top_count, table_ref, slots_ref, z_ref, x_ref):
    src = pl.program_id(0)
    n_tok = z_ref.shape[0]
    total = table_ref[3 * n_src * n_local + n_local + src]

    def chunk(c, carry):
        base = c * ROWS
        rows = lax.broadcasted_iota(jnp.int32, (ROWS, n_tok), 0) + base
        hit = rows == slots_ref[0, 0:1, :]
        for j in range(1, top_count):
            hit = hit | (rows == slots_ref[0, j : j + 1, :])
        pick = jnp.where(hit, 1.0, 0.0).astype(jnp.bfloat16)
        got = jnp.dot(pick, z_ref[...], preferred_element_type=jnp.float32)
        x_ref[0, pl.ds(pl.multiple_of(base, ROWS), ROWS), :] = got.astype(jnp.bfloat16)
        return carry

    lax.fori_loop(0, (total + ROWS - 1) // ROWS, chunk, 0)


def gather_rows(table, slot_rows, z_all, n_local, top_count, max_rows):
    n_src = slot_rows.shape[0]
    n_tok = z_all.shape[0] // n_src
    d_model = z_all.shape[1]
    return pl.pallas_call(
        functools.partial(gather_kernel, n_src, n_local, top_count),
        out_shape=jax.ShapeDtypeStruct((n_src, max_rows, d_model), jnp.bfloat16),
        grid_spec=pltpu.PrefetchScalarGridSpec(
            num_scalar_prefetch=1,
            grid=(n_src,),
            in_specs=[
                pl.BlockSpec((1, 8, n_tok), lambda s, t: (s, 0, 0)),
                pl.BlockSpec((n_tok, d_model), lambda s, t: (s, 0)),
            ],
            out_specs=pl.BlockSpec((1, max_rows, d_model), lambda s, t: (s, 0, 0)),
        ),
        compiler_params=pltpu.CompilerParams(dimension_semantics=("arbitrary",), vmem_limit_bytes=VMEM_LIMIT),
        cost_estimate=pl.CostEstimate(flops=2 * 6656 * n_tok * d_model, bytes_accessed=60_000_000, transcendentals=0),
        name="gather_rows",
    )(table, slot_rows, z_all)


def expert_kernel(n_src, n_local, table_ref, x_hbm, ga, ua, da, gb, ub, db, y_hbm, x_buf, y_buf, in_sems, out_sems):
    step = pl.program_id(0)
    n_seg = n_src * n_local
    bits = in_sems.shape[2]

    def pieces(which, act):
        slot = lax.rem(which, 2)
        for s in range(n_src):
            off = table_ref[s * n_local + which]
            size = table_ref[n_seg + s * n_local + which]
            place = table_ref[2 * n_seg + s * n_local + which]
            units = size // SEG
            done = 0
            for b in reversed(range(bits)):
                length = SEG << b
                at_hbm = pl.multiple_of(off + done, SEG)
                at_buf = pl.multiple_of(place + done, SEG)
                has = (units >> b) & 1

                @pl.when(has == 1)
                def _():
                    act(slot, s, b, at_hbm, at_buf, length)

                done = done + has * length

    def in_copy(slot, s, b, at_hbm, at_buf, length):
        return pltpu.make_async_copy(x_hbm.at[s, pl.ds(at_hbm, length)], x_buf.at[slot, pl.ds(at_buf, length)], in_sems.at[slot, s, b])

    def out_copy(slot, s, b, at_hbm, at_buf, length):
        return pltpu.make_async_copy(y_buf.at[slot, pl.ds(at_buf, length)], y_hbm.at[s, pl.ds(at_hbm, length)], out_sems.at[slot, s, b])

    @pl.when(step == 0)
    def _():
        pieces(step, lambda *a: in_copy(*a).start())

    @pl.when(step + 1 < n_local)
    def _():
        pieces(step + 1, lambda *a: in_copy(*a).start())

    pieces(step, lambda *a: in_copy(*a).wait())

    @pl.when(step >= 2)
    def _():
        pieces(step - 2, lambda *a: out_copy(*a).wait())

    slot = lax.rem(step, 2)
    total = table_ref[3 * n_seg + step]
    n_blocks = (total + ROWS - 1) // ROWS

    def run(gate, up, down):
        def block(c, carry):
            rows = pl.ds(pl.multiple_of(c * ROWS, ROWS), ROWS)
            x = x_buf[slot, rows, :]
            g = jnp.dot(x, gate[0], preferred_element_type=jnp.float32)
            u = jnp.dot(x, up[0], preferred_element_type=jnp.float32)
            h = (g * jax.nn.sigmoid(g) * u).astype(jnp.bfloat16)
            y_buf[slot, rows, :] = jnp.dot(h, down[0], preferred_element_type=jnp.float32).astype(jnp.bfloat16)
            return carry

        lax.fori_loop(0, n_blocks, block, 0)

    @pl.when(step < n_local // 2)
    def _():
        run(ga, ua, da)

    @pl.when(step >= n_local // 2)
    def _():
        run(gb, ub, db)

    pieces(step, lambda *a: out_copy(*a).start())

    @pl.when(step == n_local - 1)
    def _():
        pieces(step - 1, lambda *a: out_copy(*a).wait())
        pieces(step, lambda *a: out_copy(*a).wait())


def expert_rows(table, x_rows, own, other, slot_cap):
    n_src, max_rows, d_model = x_rows.shape
    half, _, width = own[0].shape
    n_local = 2 * half
    buf_rows = -(-n_src * slot_cap // ROWS) * ROWS
    bits = (slot_cap // SEG).bit_length()
    own_at = lambda l, t: (jnp.minimum(l, half - 1), 0, 0)
    other_at = lambda l, t: (jnp.maximum(l - half, 0), 0, 0)
    return pl.pallas_call(
        functools.partial(expert_kernel, n_src, n_local),
        out_shape=jax.ShapeDtypeStruct(x_rows.shape, jnp.bfloat16),
        grid_spec=pltpu.PrefetchScalarGridSpec(
            num_scalar_prefetch=1,
            grid=(n_local,),
            in_specs=[
                pl.BlockSpec(memory_space=pl.ANY),
                pl.BlockSpec((1, d_model, width), own_at),
                pl.BlockSpec((1, d_model, width), own_at),
                pl.BlockSpec((1, width, d_model), own_at),
                pl.BlockSpec((1, d_model, width), other_at),
                pl.BlockSpec((1, d_model, width), other_at),
                pl.BlockSpec((1, width, d_model), other_at),
            ],
            out_specs=pl.BlockSpec(memory_space=pl.ANY),
            scratch_shapes=[
                pltpu.VMEM((2, buf_rows, d_model), jnp.bfloat16),
                pltpu.VMEM((2, buf_rows, d_model), jnp.bfloat16),
                pltpu.SemaphoreType.DMA((2, n_src, bits)),
                pltpu.SemaphoreType.DMA((2, n_src, bits)),
            ],
        ),
        compiler_params=pltpu.CompilerParams(dimension_semantics=("arbitrary",), vmem_limit_bytes=VMEM_LIMIT),
        cost_estimate=pl.CostEstimate(flops=2 * 8192 * d_model * width * 3, bytes_accessed=115_000_000, transcendentals=0),
        name="expert_rows",
    )(table, x_rows, *own, *other)


def combine_kernel(n_src, n_local, top_count, table_ref, cols_ref, y_ref, out_ref, slot_bc, weight_bc):
    src = pl.program_id(0)
    n_tok = out_ref.shape[0]
    total = table_ref[3 * n_src * n_local + n_local + src]
    lanes = 128
    for j in range(top_count):
        slot_bc[j] = jnp.broadcast_to(cols_ref[0, :, j : j + 1], (n_tok, lanes))
        weight_bc[j] = jnp.broadcast_to(cols_ref[0, :, top_count + j : top_count + j + 1], (n_tok, lanes))
    out_ref[...] = jnp.zeros_like(out_ref)

    def chunk(c, carry):
        base = c * ROWS
        rows = pl.ds(pl.multiple_of(base, ROWS), ROWS)
        y = y_ref[0, rows, :]
        y_at = lax.broadcasted_iota(jnp.int32, y.shape, 0) + base
        y = jnp.where(y_at < total, y, jnp.zeros_like(y))

        def tokens(i, inner):
            tok = pl.ds(pl.multiple_of(i * ROWS, ROWS), ROWS)
            parts = [[], [], []]
            for half in range(ROWS // lanes):
                lane_at = (lax.broadcasted_iota(jnp.int32, (ROWS, lanes), 1) + (base + half * lanes)).astype(jnp.float32)
                coef = jnp.zeros((ROWS, lanes), jnp.float32)
                for j in range(top_count):
                    coef = jnp.where(slot_bc[j, tok, :] == lane_at, weight_bc[j, tok, :], coef)
                high = coef.astype(jnp.bfloat16)
                rest = coef - high.astype(jnp.float32)
                mid = rest.astype(jnp.bfloat16)
                low = (rest - mid.astype(jnp.float32)).astype(jnp.bfloat16)
                for part, val in zip(parts, (high, mid, low)):
                    part.append(val)
            high, mid, low = (jnp.concatenate(part, axis=1) for part in parts)
            acc = jnp.dot(low, y, preferred_element_type=jnp.float32)
            acc = acc + jnp.dot(mid, y, preferred_element_type=jnp.float32)
            acc = acc + jnp.dot(high, y, preferred_element_type=jnp.float32)
            out_ref[tok, :] += acc
            return inner

        lax.fori_loop(0, n_tok // ROWS, tokens, 0)
        return carry

    lax.fori_loop(0, (total + ROWS - 1) // ROWS, chunk, 0)


def combine_rows(table, cols, y_rows, n_local, top_count):
    n_src, max_rows, d_model = y_rows.shape
    n_tok = cols.shape[1]
    return pl.pallas_call(
        functools.partial(combine_kernel, n_src, n_local, top_count),
        out_shape=jax.ShapeDtypeStruct((n_src * n_tok, d_model), jnp.float32),
        grid_spec=pltpu.PrefetchScalarGridSpec(
            num_scalar_prefetch=1,
            grid=(n_src,),
            in_specs=[
                pl.BlockSpec((1, n_tok, 2 * top_count), lambda s, t: (s, 0, 0)),
                pl.BlockSpec((1, max_rows, d_model), lambda s, t: (s, 0, 0)),
            ],
            out_specs=pl.BlockSpec((n_tok, d_model), lambda s, t: (s, 0)),
            scratch_shapes=[
                pltpu.VMEM((top_count, n_tok, 128), jnp.float32),
                pltpu.VMEM((top_count, n_tok, 128), jnp.float32),
            ],
        ),
        compiler_params=pltpu.CompilerParams(dimension_semantics=("arbitrary",), vmem_limit_bytes=VMEM_LIMIT),
        cost_estimate=pl.CostEstimate(flops=6 * 7168 * n_tok * d_model, bytes_accessed=62_000_000, transcendentals=0),
        name="combine_rows",
    )(table, cols, y_rows)


def solution(mesh):
    group_size = mesh.shape["ep"]
    n_src = group_size // 2
    ring_groups = [[2 * k + core for k in range(n_src)] for core in range(2)]
    pair_perm = [(k, k ^ 1) for k in range(group_size)]

    def device_step(tokens, expert_ids, route_weights, attn_norm, w_query, w_key, w_value, w_out, ffn_norm, w_gate, w_up, w_down, shared_gate, shared_up, shared_down):
        n_micro, n_seq, seq_len, d_model = tokens.shape
        n_tok = n_seq * seq_len
        top_count = expert_ids.shape[-1]
        half = w_gate.shape[0]
        n_local = 2 * half
        slot_cap = capacity_of(n_tok, top_count, half * group_size)
        max_rows = n_local * slot_cap
        me = lax.axis_index("ep")

        own = (w_gate, w_up, w_down)
        other = tuple(lax.ppermute(w, "ep", pair_perm) for w in own)

        meta = jnp.concatenate([expert_ids.astype(jnp.float32).transpose(0, 2, 1), route_weights.transpose(0, 2, 1), jnp.zeros((n_micro, 16 - 2 * top_count, n_tok), jnp.float32)], axis=1)
        meta = lax.all_gather(meta.reshape(n_micro * 16, n_tok), "ep", axis=0, tiled=True)
        meta = meta.reshape(n_src, 2, n_micro, 16, n_tok)
        meta = lax.dynamic_index_in_dim(meta, me % 2, axis=1, keepdims=False)
        ids = meta[:, :, :top_count].astype(jnp.int32)
        all_weights = meta[:, :, top_count : 2 * top_count]
        from_own = ids - half * me
        from_other = ids - half * (me ^ 1)
        local_ids = jnp.where((from_own >= 0) & (from_own < half), from_own, jnp.where((from_other >= 0) & (from_other < half), from_other + half, -1))
        plans = [route_tables(local_ids[:, m], all_weights[:, m], n_local) for m in range(n_micro)]

        residuals, normeds, gathered = [], [], []
        for m in range(n_micro):
            residual = attention_block(tokens[m], attn_norm, w_query, w_key, w_value, w_out).reshape(n_tok, d_model)
            normed = rms_norm(residual, ffn_norm)
            residuals.append(residual)
            normeds.append(normed)
            gathered.append(lax.all_gather(normed, "ep", axis=0, tiled=True, axis_index_groups=ring_groups))
        outs = []
        for m in range(n_micro):
            table, slot_rows, cols = plans[m]
            x_rows = gather_rows(table, slot_rows, gathered[m], n_local, top_count, max_rows)
            y_rows = expert_rows(table, x_rows, own, other, slot_cap)
            partial = combine_rows(table, cols, y_rows, n_local, top_count)
            routed = lax.psum_scatter(partial, "ep", scatter_dimension=0, tiled=True, axis_index_groups=ring_groups)
            shared_out = swiglu(normeds[m], shared_gate, shared_up, shared_down)
            layer_rows = residuals[m].astype(jnp.float32) + shared_out.astype(jnp.float32) + routed
            outs.append(layer_rows.astype(jnp.bfloat16).reshape(n_seq, seq_len, d_model))
        return jnp.stack(outs)

    token_spec = P(None, ("dp", "ep"), None, None)
    route_spec = P(None, ("dp", "ep"), None)
    rep_spec = P()
    expert_spec = P("ep", None, None)
    in_specs = (token_spec, route_spec, route_spec, rep_spec, rep_spec, rep_spec, rep_spec, rep_spec, rep_spec, expert_spec, expert_spec, expert_spec, rep_spec, rep_spec, rep_spec)
    return jax.shard_map(device_step, mesh=mesh, in_specs=in_specs, out_specs=token_spec, check_vma=False)
```

time: 2440 us -> 1010 us (0.41)
  local copies, waits for them, and re-layouts: 752 us -> 17.9 us
  waiting for transfers between devices: 830 us -> 291 us
  Pallas kernels: 0 us -> 441 us
  other arithmetic: 488 us -> 100 us
  matrix products: 321 us -> 142 us
  starting transfers between devices: 31.6 us -> 1.31 us
    all_to_all x4 -> x0, waiting for transfers between devices: 830 us -> none  [the longest x2 478 us: device_step(): recv_rows = lax.all_to_all(send_rows, 'ep', 0, 0, tiled=True)]
    gather x14 -> x0, local copies, waits for them, and re-layouts: 556 us -> none  [the longest x2 263 us: device_step(): jnp.take(back_rows.reshape(experts * slot_cap, d_model), flat_ids * slot_...]
    pallas_call x0 -> x6, Pallas kernels: none -> 441 us  [the longest x2 227 us: combine_rows(): pl.pallas_call(functools.partial(combine_kernel, n_src, n_local, top_coun...]
    reduce_scatter x0 -> x2, waiting for transfers between devices: none -> 193 us  [device_step(): lax.psum_scatter(partial, 'ep', scatter_dimension=0, tiled=True, axis_ind...]
    dot_general x4 -> x2, matrix products: 178 us -> 0.76 us  [route_tables(): jnp.dot(mask.astype(jnp.bfloat16).reshape(n_src * n_local, n_tok), upper,...]
    convert_element_type x4 -> x0, local copies, waits for them, and re-layouts: 136 us -> none  [the longest x2 83.7 us: device_step(): picked.astype(jnp.float32) * route_weights[micro_idx][:, :, None]]
    reduce_sum x2 -> x4, other arithmetic: 129 us -> 1.61 us  [the longest x1 0.71 us: route_tables(): slots = jnp.sum(jnp.where(hits, slot_of[:, None] + 1, 0), axis=2) - 1]
    all_gather x0 -> x3, waiting for transfers between devices: none -> 97.7 us  [the longest x2 97.7 us: device_step(): lax.all_gather(normed, 'ep', axis=0, tiled=True, axis_index_groups=ring_g...]
  transfers between devices with their start and end apart: 4 -> 8, of which waited for: 4 -> 2; matrix products, arithmetic and copies ran while one was open for 33% -> 25% of each run, Pallas kernels for 0% -> 44%
where the time goes in v1:
time: 1010 us
  Pallas kernels  441 us (44%)
  waiting for transfers between devices  291 us (29%)
  matrix products  142 us (14%)
  other arithmetic  100 us (10%)
  local copies, waits for them, and re-layouts  17.9 us (2%)
  between operations  14 us (1%)
    pallas_call x2, Pallas kernels, combine_rows(): pl.pallas_call(functools.partial(combine_kernel, n_src, n_local, top_coun...  227 us
    reduce_scatter x2, waiting for transfers between devices, device_step(): lax.psum_scatter(partial, 'ep', scatter_dimension=0, tiled=True, axis_ind...  193 us
    pallas_call x2, Pallas kernels, expert_rows(): pl.pallas_call(functools.partial(expert_kernel, n_src, n_local), out_shap...  124 us
    all_gather x2, waiting for transfers between devices, device_step(): lax.all_gather(normed, 'ep', axis=0, tiled=True, axis_index_groups=ring_g...  97.7 us
    pallas_call x2, Pallas kernels, gather_rows(): pl.pallas_call(functools.partial(gather_kernel, n_src, n_local, top_count...  89.7 us
    sub x2, other arithmetic, attention_block(): jax.nn.softmax(jnp.where(causal, scores, -jnp.inf), axis=-1)  57.6 us
    dot_general x2, matrix products, attention_block(): jnp.einsum('...qhe,...khe->...hqk', queries, key_rows, preferred_element_...  33.4 us
    dot_general x2, matrix products, attention_block(): jnp.einsum('...hqk,...khe->...qhe', attn_probs, value_rows, preferred_ele...  33 us
  transfers between devices with their start and end apart: 8, of which 2 were waited for; matrix products, arithmetic and copies ran while one was open for 25% of the time, Pallas kernels for 44%

profile of v1, /device:TPU:112, one launch (start us, length us, event | category | flops | bytes accessed | tf_op | source)
XLA Modules:
  0.0 1007.3 jit_solution(12330123010512646978)
XLA Ops:
  14.4 7.7 fusion.40
  22.1 16.6 %fusion.66 = f32[2,12,512,512]{2,3,1,0:T(8,128)} fusion(bf16[1536,12,128]{2,0,1:T(8,128)(2,1)} %param.20, bf16[2,512,12,128]{3,1,2,0:T(8,128)(2,1)S(1)} %fusion.40, f32[1536]{0:T(1024)S(1)} %convert_element_type.164, f32[2,512]{1,0:T(2,128)S(1)} %get-tuple-element.45, bf16[2,2,512,1536]{3,2,1,0:T(8,128)(2,1)} %param.15), kind=kOutput, calls=%fused_computation.82 | convolution fusion | flops 6450315264 | bytes 36186112 | tf_op jit(solution)/shard_map/...qhe,...khe->...hqk/dot_general | solution.py:34
  38.7 28.6 %fusion.130 = (f32[2,12,512]{2,1,0:T(8,128)S(1)}, f32[2,12,512,512]{2,3,1,0:T(8,128)}) fusion(f32[2,12,512,512]{2,3,1,0:T(8,128)} %fusion.66, pred[512,512]{0,1:T(8,128)(4,1)S(1)} %iota_compare_fusion.9), kind=kOutput, calls=%fused_computation.184 | output fusion | flops 37749248 | bytes 50642944 | tf_op jit(solution)/shard_map/sub | solution.py:36
  67.3 16.6 %fusion.8 = bf16[2,12,128,512]{3,2,1,0:T(8,128)(2,1)} fusion(f32[2,12,512,512]{2,3,1,0:T(8,128)} %get-tuple-element.32, f32[2,12,512]{2,1,0:T(8,128)S(1)} %get-tuple-element.31, bf16[1536,12,128]{2,0,1:T(8,128)(2,1)} %param.21, f32[1536]{0:T(1024)S(1)} %convert_element_type.164, f32[2,512]{1,0:T(2,128)S(1)} %get-tuple-element.45, ...), kind=kOutput, calls=%fused_computation.14 | convolution fusion | flops 6462898176 | bytes 36235264 | tf_op jit(solution)/shard_map/...hqk,...khe->...qhe/dot_general | solution.py:37
  83.8 9.2 fusion.25
  93.1 10.4 %fusion.38 = bf16[2,512,12,128]{3,1,2,0:T(8,128)(2,1)} fusion(bf16[1536,12,128]{2,0,1:T(8,128)(2,1)} %param.19, f32[2,512]{1,0:T(2,128)S(1)} %get-tuple-element.44, f32[1536]{0:T(1024)S(1)} %convert_element_type.164, bf16[2,2,512,1536]{3,2,1,0:T(8,128)(2,1)} %param.15), kind=kOutput, calls=%fused_computation.57 | convolution fusion | flops 4838129664 | bytes 11020288 | tf_op jit(solution)/shard_map/...sd,dhe->...she/dot_general | solution.py:30
  103.4 16.8 %fusion.57 = f32[2,12,512,512]{2,3,1,0:T(8,128)} fusion(bf16[1536,12,128]{2,0,1:T(8,128)(2,1)} %param.20, bf16[2,512,12,128]{3,1,2,0:T(8,128)(2,1)} %fusion.38, f32[2,512]{1,0:T(2,128)S(1)} %get-tuple-element.44, f32[1536]{0:T(1024)S(1)} %convert_element_type.164, bf16[2,2,512,1536]{3,2,1,0:T(8,128)(2,1)} %param.15), kind=kOutput, calls=%fused_computation.77 | convolution fusion | flops 6450315264 | bytes 36186112 | tf_op jit(solution)/shard_map/...qhe,...khe->...hqk/dot_general | solution.py:34
  120.3 29.0 %fusion.131 = (f32[2,12,512]{2,1,0:T(8,128)S(1)}, f32[2,12,512,512]{2,3,1,0:T(8,128)}) fusion(f32[2,12,512,512]{2,3,1,0:T(8,128)} %fusion.57, pred[512,512]{0,1:T(8,128)(4,1)S(1)} %iota_compare_fusion.9), kind=kOutput, calls=%fused_computation.185 | output fusion | flops 37749248 | bytes 50642944 | tf_op jit(solution)/shard_map/sub | solution.py:36
  149.3 16.4 %fusion.9 = bf16[2,12,128,512]{3,2,1,0:T(8,128)(2,1)} fusion(f32[2,12,512,512]{2,3,1,0:T(8,128)} %get-tuple-element.36, f32[2,12,512]{2,1,0:T(8,128)S(1)} %get-tuple-element.35, bf16[1536,12,128]{2,0,1:T(8,128)(2,1)} %param.21, f32[2,512]{1,0:T(2,128)S(1)} %get-tuple-element.44, f32[1536]{0:T(1024)S(1)} %convert_element_type.164, ...), kind=kOutput, calls=%fused_computation.15 | convolution fusion | flops 6462898176 | bytes 36235264 | tf_op jit(solution)/shard_map/...hqk,...khe->...qhe/dot_general | solution.py:37
  165.7 9.2 fusion.20
  198.8 97.7 %all-gather.8.cloned.1.call-done.z_ref = bf16[4096,1536]{1,0:T(8,128)(2,1)} async-done(((bf16[1024,1536]{1,0:T(8,128)(2,1)}), bf16[4096,1536]{1,0:T(8,128)(2,1)}) %all-gather.8.cloned.1.call-update) | async-done | bytes 12582928 | tf_op jit(solution)/shard_map/all_gather | solution.py:331
  296.5 44.9 %gather_rows.3.x_hbm = bf16[4,3072,1536]{2,1,0:T(8,128)(2,1)} custom-call(s32[212]{0:T(256)} %concatenate.25.table_ref, s32[4,8,1024]{2,1,0:T(8,128)} %concatenate.27.clone.slots_ref, bf16[4096,1536]{1,0:T(8,128)(2,1)} %all-gather.8.cloned.1.call-done.z_ref), custom_call_target="tpu_custom_call" | custom-call | flops 20937965568 | bytes 60000000 | tf_op jit(solution)/shard_map/gather_rows/pallas_call | solution.py:94
  341.4 62.0 %expert_rows.3.y_ref = bf16[4,3072,1536]{2,1,0:T(8,128)(2,1)} custom-call(s32[212]{0:T(256)} %concatenate.25.table_ref, bf16[4,3072,1536]{2,1,0:T(8,128)(2,1)} %gather_rows.3.x_hbm, bf16[8,1536,512]{2,1,0:T(8,128)(2,1)} %ga.3, bf16[8,1536,512]{2,1,0:T(8,128)(2,1)} %ua.3, bf16[8,512,1536]{2,1,0:T(8,128)(2,1)} %da.3, ...), custom_call_target="tpu_custom_call" | custom-call | flops 38654705664 | bytes 115000000 | tf_op jit(solution)/shard_map/expert_rows/pallas_call | solution.py:197
  403.4 113.8 %combine_rows.3 = f32[4096,1536]{1,0:T(8,128)} custom-call(s32[212]{0:T(256)} %concatenate.25.table_ref, f32[4,1024,12]{2,1,0:T(8,128)} %maximum_bitcast_fusion.1.cols_ref, bf16[4,3072,1536]{2,1,0:T(8,128)(2,1)} %expert_rows.3.y_ref), custom_call_target="tpu_custom_call" | custom-call | flops 67645734912 | bytes 62000000 | tf_op jit(solution)/shard_map/combine_rows/pallas_call | solution.py:273
  532.0 44.9 %gather_rows.2.x_hbm = bf16[4,3072,1536]{2,1,0:T(8,128)(2,1)} custom-call(s32[212]{0:T(256)} %concatenate.22.table_ref, s32[4,8,1024]{2,1,0:T(8,128)} %concatenate.24.clone.slots_ref, bf16[4096,1536]{1,0:T(8,128)(2,1)} %all-gather.6.cloned.1.call-done.z_ref), custom_call_target="tpu_custom_call" | custom-call | flops 20937965568 | bytes 60000000 | tf_op jit(solution)/shard_map/gather_rows/pallas_call | solution.py:94
  576.9 62.3 %expert_rows.2.y_ref = bf16[4,3072,1536]{2,1,0:T(8,128)(2,1)} custom-call(s32[212]{0:T(256)} %concatenate.22.table_ref, bf16[4,3072,1536]{2,1,0:T(8,128)(2,1)} %gather_rows.2.x_hbm, bf16[8,1536,512]{2,1,0:T(8,128)(2,1)} %ga.3, bf16[8,1536,512]{2,1,0:T(8,128)(2,1)} %ua.3, bf16[8,512,1536]{2,1,0:T(8,128)(2,1)} %da.3, ...), custom_call_target="tpu_custom_call" | custom-call | flops 38654705664 | bytes 115000000 | tf_op jit(solution)/shard_map/expert_rows/pallas_call | solution.py:197
  639.2 113.7 %combine_rows.2 = f32[4096,1536]{1,0:T(8,128)} custom-call(s32[212]{0:T(256)} %concatenate.22.table_ref, f32[4,1024,12]{2,1,0:T(8,128)} %maximum_bitcast_fusion.cols_ref, bf16[4,3072,1536]{2,1,0:T(8,128)(2,1)} %expert_rows.2.y_ref), custom_call_target="tpu_custom_call" | custom-call | flops 67645734912 | bytes 62000000 | tf_op jit(solution)/shard_map/combine_rows/pallas_call | solution.py:273
  753.0 8.4 fusion.133
  761.4 5.0 fusion.132
  766.4 12.3 %convolution_convert_fusion = bf16[1024,1536]{1,0:T(8,128)(2,1)} fusion(bf16[1024,1536]{1,0:T(8,128)(2,1)} %param.29, f32[1024,1024]{1,0:T(8,128)} %fusion.133, bf16[1024,1536]{1,0:T(8,128)(2,1)} %get-tuple-element.26, bf16[1536,1024]{1,0:T(8,128)(2,1)} %param.28), kind=kOutput, calls=%fused_computation.70 | convolution fusion | flops 6450315264 | bytes 16777216 | tf_op jit(solution)/shard_map/dot_general | solution.py:46
  778.7 12.4 %convolution_convert_fusion.1 = bf16[1024,1536]{1,0:T(8,128)(2,1)} fusion(bf16[1024,1536]{1,0:T(8,128)(2,1)} %param.29, f32[1024,1024]{1,0:T(8,128)} %fusion.132, bf16[1024,1536]{1,0:T(8,128)(2,1)S(1)} %copy-done.1, bf16[1536,1024]{1,0:T(8,128)(2,1)} %param.28), kind=kOutput, calls=%fused_computation.71 | convolution fusion | flops 6450315264 | bytes 16777216 | tf_op jit(solution)/shard_map/dot_general | solution.py:46
  791.1 7.7 fusion.24
  798.8 193.1 %reduce-scatter.3.cloned.1.call-done = f32[1024,1536]{1,0:T(8,128)} async-done(((f32[4096,1536]{1,0:T(8,128)}), f32[1024,1536]{1,0:T(8,128)}) %reduce-scatter.3.cloned.1.call-update) | async-done | bytes 6291472 | tf_op jit(solution)/shard_map/reduce_scatter | solution.py:338
  991.9 5.1 fusion.29
  (101 shorter events, 49.8 us)
Async XLA Ops:
  6.5 7.3 copy-start.7
  6.5 173.1 %all-gather.4.cloned.1.call-start = ((), (), s32[]{:S(2)}) async-start(), calls=%async_computation.2 | async-start | bytes 1179648 | tf_op jit(solution)/shard_map/all_gather | solution.py:315
  9.1 287.4 %all-gather.8.cloned.1.call-start = ((), (), s32[]{:S(2)}) async-start(), calls=%async_computation.5 | async-start | bytes 15728640 | tf_op jit(solution)/shard_map/all_gather | solution.py:331
  9.2 5.3 copy-start
  93.0 81.9 %copy-start.2 = (bf16[2,512,1536]{2,1,0:T(8,128)(2,1)}, bf16[2,512,1536]{2,1,0:T(8,128)(2,1)S(1)}, u32[]{:S(2)}) copy-start(bf16[2,512,1536]{2,1,0:T(8,128)(2,1)S(1)} %get-tuple-element.34) | copy-start | bytes 9437188
  165.7 9.2 copy-start.6
  174.8 3.6 copy-start.4
  178.5 353.6 %all-gather.6.cloned.1.call-start = ((), (), s32[]{:S(2)}) async-start(), calls=%async_computation.3 | async-start | bytes 15728640 | tf_op jit(solution)/shard_map/all_gather | solution.py:331
  178.6 162.8 %collective-permute-start = (bf16[8,1536,512]{2,1,0:T(8,128)(2,1)}, bf16[8,1536,512]{2,1,0:T(8,128)(2,1)}, u32[]{:S(2)}, u32[]{:S(2)}) collective-permute-start(bf16[8,1536,512]{2,1,0:T(8,128)(2,1)} %ga.3), channel_id=1, source_target_pairs={{0,1},{1,0},{2,3},{3,2},{4,5},{5,4},{6,7},{7,6},{8,9},{9,8},{10,11... | collective-permute-start | bytes 37748744 | tf_op jit(solution)/shard_map/ppermute | solution.py:312
  178.7 162.7 %collective-permute-start.1 = (bf16[8,1536,512]{2,1,0:T(8,128)(2,1)}, bf16[8,1536,512]{2,1,0:T(8,128)(2,1)}, u32[]{:S(2)}, u32[]{:S(2)}) collective-permute-start(bf16[8,1536,512]{2,1,0:T(8,128)(2,1)} %ua.3), channel_id=1, source_target_pairs={{0,1},{1,0},{2,3},{3,2},{4,5},{5,4},{6,7},{7,6},{8,9},{9,8},{10,11... | collective-permute-start | bytes 37748744 | tf_op jit(solution)/shard_map/ppermute | solution.py:312
  179.1 162.2 %collective-permute-start.2 = (bf16[8,512,1536]{2,1,0:T(8,128)(2,1)}, bf16[8,512,1536]{2,1,0:T(8,128)(2,1)}, u32[]{:S(2)}, u32[]{:S(2)}) collective-permute-start(bf16[8,512,1536]{2,1,0:T(8,128)(2,1)} %da.3), channel_id=1, source_target_pairs={{0,1},{1,0},{2,3},{3,2},{4,5},{5,4},{6,7},{7,6},{8,9},{9,8},{10,11... | collective-permute-start | bytes 37748744 | tf_op jit(solution)/shard_map/ppermute | solution.py:312
  179.3 611.8 %reduce-scatter.5.cloned.1.call-start = ((), (), s32[]{:S(2)}) async-start(), calls=%async_computation.6 | async-start | bytes 31457280 | tf_op jit(solution)/shard_map/reduce_scatter | solution.py:338
  517.2 474.7 %reduce-scatter.3.cloned.1.call-start = ((), (), s32[]{:S(2)}) async-start(), calls=%async_computation.4 | async-start | bytes 31457280 | tf_op jit(solution)/shard_map/reduce_scatter | solution.py:338
  521.7 6.1 copy-start.8
  521.7 6.1 copy-start.9
  753.0 8.4 copy-start.1
  753.0 8.4 copy-start.10
  791.1 200.8 %copy-start.3 = (bf16[2,512,1536]{2,1,0:T(8,128)(2,1)S(1)}, bf16[2,512,1536]{2,1,0:T(8,128)(2,1)}, u32[]{:S(2)}) copy-start(bf16[2,512,1536]{2,1,0:T(8,128)(2,1)} %copy-done.2) | copy-start | bytes 9437188
  991.9 5.2 copy-start.5
Sparse Core Ops, SparseCore 0:
  9.2 21.8 all-gather.3
  178.6 117.8 all-gather.7
  298.1 115.9 all-gather.5
  517.3 236.6 reduce-scatter.4
  756.2 235.6 reduce-scatter.2

commit v2 on v1

--- a/solution.py
+++ b/solution.py
@@ -7,6 +7,7 @@
 from jax.experimental.pallas import tpu as pltpu
 from jax.sharding import PartitionSpec as P
 
+
 NORM_EPS = 1e-6
 CAP_FACTOR = 2
 SLOT_ALIGN = 8
@@ -25,18 +26,70 @@
     return (wide_vals * inv_rms * norm_gain.astype(jnp.float32)).astype(jnp.bfloat16)
 
 
-def attention_block(seq_rows, attn_norm, w_query, w_key, w_value, w_out):
-    normed = rms_norm(seq_rows, attn_norm)
-    queries = jnp.einsum("...sd,dhe->...she", normed, w_query, preferred_element_type=jnp.float32).astype(jnp.bfloat16)
-    key_rows = jnp.einsum("...sd,dhe->...she", normed, w_key, preferred_element_type=jnp.float32).astype(jnp.bfloat16)
-    value_rows = jnp.einsum("...sd,dhe->...she", normed, w_value, preferred_element_type=jnp.float32).astype(jnp.bfloat16)
-    seq_len = seq_rows.shape[-2]
-    scores = jnp.einsum("...qhe,...khe->...hqk", queries, key_rows, preferred_element_type=jnp.float32) * (w_query.shape[-1] ** -0.5)
-    causal = jnp.arange(seq_len)[:, None] >= jnp.arange(seq_len)[None, :]
-    attn_probs = jax.nn.softmax(jnp.where(causal, scores, -jnp.inf), axis=-1).astype(jnp.bfloat16)
-    head_mix = jnp.einsum("...hqk,...khe->...qhe", attn_probs, value_rows, preferred_element_type=jnp.float32).astype(jnp.bfloat16)
-    attn_out = jnp.einsum("...qhe,hed->...qd", head_mix, w_out, preferred_element_type=jnp.float32)
-    return (seq_rows.astype(jnp.float32) + attn_out).astype(jnp.bfloat16)
+def attention_kernel(gain_ref, ffn_gain_ref, x_ref, wq_ref, wk_ref, wv_ref, wo_ref, h_ref, z_ref, normed, acc):
+    group, seq = pl.program_id(0), pl.program_id(1)
+    seq_len, d_model = normed.shape[1:]
+    per, _, head_dim = wq_ref.shape
+    block = seq_len // 2
+
+    @pl.when(group == 0)
+    def _():
+        normed[seq] = rms_norm(x_ref[0, seq], gain_ref[...])
+
+    rows = normed[seq]
+    project = lambda w_ref: jnp.dot(rows, jnp.concatenate([w_ref[i] for i in range(per)], axis=1), preferred_element_type=jnp.float32).astype(jnp.bfloat16)
+    queries, key_rows, value_rows = project(wq_ref), project(wk_ref), project(wv_ref)
+    above = lax.broadcasted_iota(jnp.int32, (block, block), 0) < lax.broadcasted_iota(jnp.int32, (block, block), 1)
+    tops, ends = [], []
+    for i in range(per):
+        lanes = slice(i * head_dim, (i + 1) * head_dim)
+        k, v = key_rows[:, lanes], value_rows[:, lanes]
+        for part, outs in ((0, tops), (1, ends)):
+            q = queries[part * block : (part + 1) * block, lanes]
+            scores = lax.dot_general(q, k[: (part + 1) * block], (((1,), (1,)), ((), ())), preferred_element_type=jnp.float32) * (head_dim**-0.5)
+            diag = jnp.where(above, -jnp.inf, scores[:, part * block :])
+            scores = diag if part == 0 else jnp.concatenate([scores[:, :block], diag], axis=1)
+            shifted = jnp.exp(scores - jnp.max(scores, axis=1, keepdims=True))
+            probs = (shifted * (1.0 / jnp.sum(shifted, axis=1, keepdims=True))).astype(jnp.bfloat16)
+            outs.append(jnp.dot(probs, v[: (part + 1) * block], preferred_element_type=jnp.float32).astype(jnp.bfloat16))
+    mix = jnp.concatenate([jnp.concatenate(tops, axis=1), jnp.concatenate(ends, axis=1)], axis=0)
+    added = jnp.dot(mix, wo_ref[...].reshape(per * head_dim, d_model), preferred_element_type=jnp.float32)
+
+    @pl.when(group == 0)
+    def _():
+        acc[seq] = added
+
+    @pl.when(group > 0)
+    def _():
+        acc[seq] += added
+
+    @pl.when(group == pl.num_programs(0) - 1)
+    def _():
+        residual = (x_ref[0, seq].astype(jnp.float32) + acc[seq]).astype(jnp.bfloat16)
+        h_ref[seq] = residual
+        z_ref[seq] = rms_norm(residual, ffn_gain_ref[...])
+
+
+def attention_rows(tokens, micro, first, n_seq, gains, weights):
+    _, _, seq_len, d_model = tokens.shape
+    n_heads, _, head_dim = weights[0].shape
+    per = 2
+    out = jax.ShapeDtypeStruct((n_seq, seq_len, d_model), jnp.bfloat16)
+    whole = pl.BlockSpec((n_seq, seq_len, d_model), lambda g, s: (0, 0, 0))
+    gain = pl.BlockSpec((1, d_model), lambda g, s: (0, 0))
+    in_w = pl.BlockSpec((per, d_model, head_dim), lambda g, s: (g, 0, 0))
+    rows = n_seq * seq_len
+    return pl.pallas_call(
+        attention_kernel,
+        out_shape=(out, out),
+        grid=(n_heads // per, n_seq),
+        in_specs=[gain, gain, pl.BlockSpec((1, n_seq, seq_len, d_model), lambda g, s: (micro, first // n_seq, 0, 0)), in_w, in_w, in_w, pl.BlockSpec((per, head_dim, d_model), lambda g, s: (g, 0, 0))],
+        out_specs=(whole, whole),
+        scratch_shapes=[pltpu.VMEM((n_seq, seq_len, d_model), jnp.bfloat16), pltpu.VMEM((n_seq, seq_len, d_model), jnp.float32)],
+        compiler_params=pltpu.CompilerParams(dimension_semantics=("arbitrary", "arbitrary"), vmem_limit_bytes=VMEM_LIMIT),
+        cost_estimate=pl.CostEstimate(flops=8 * rows * d_model * d_model, bytes_accessed=30_000_000, transcendentals=0),
+        name="attention_rows",
+    )(*gains, tokens, *weights)
 
 
 def swiglu(in_rows, gate_w, up_w, down_w):
@@ -68,32 +121,58 @@
     return table, slot_rows, cols
 
 
-def gather_kernel(n_src, n_local, top_count, table_ref, slots_ref, z_ref, x_ref):
+def gather_kernel(n_src, n_local, top_count, table_ref, slots_ref, z_ref, x_hbm, buf, sems, sent):
     src = pl.program_id(0)
     n_tok = z_ref.shape[0]
     total = table_ref[3 * n_src * n_local + n_local + src]
+    block = buf.shape[1]
+
+    @pl.when(src == 0)
+    def _():
+        sent[0] = 0
+
+    def copy(slot, row):
+        return pltpu.make_async_copy(buf.at[slot], x_hbm.at[src, pl.ds(row, block)], sems.at[slot])
 
     def chunk(c, carry):
-        base = c * ROWS
-        rows = lax.broadcasted_iota(jnp.int32, (ROWS, n_tok), 0) + base
-        hit = rows == slots_ref[0, 0:1, :]
-        for j in range(1, top_count):
-            hit = hit | (rows == slots_ref[0, j : j + 1, :])
-        pick = jnp.where(hit, 1.0, 0.0).astype(jnp.bfloat16)
-        got = jnp.dot(pick, z_ref[...], preferred_element_type=jnp.float32)
-        x_ref[0, pl.ds(pl.multiple_of(base, ROWS), ROWS), :] = got.astype(jnp.bfloat16)
+        base = pl.multiple_of(c * block, block)
+        slot = sent[0] & 1
+
+        @pl.when(sent[0] >= 2)
+        def _():
+            copy(slot, 0).wait()
+
+        for part in range(block // ROWS):
+            rows = lax.broadcasted_iota(jnp.int32, (ROWS, n_tok), 0) + (base + part * ROWS)
+            hit = rows == slots_ref[0, 0:1, :]
+            for j in range(1, top_count):
+                hit = hit | (rows == slots_ref[0, j : j + 1, :])
+            pick = jnp.where(hit, 1.0, 0.0).astype(jnp.bfloat16)
+            got = jnp.dot(pick, z_ref[...], preferred_element_type=jnp.float32)
+            buf[slot, part * ROWS : (part + 1) * ROWS, :] = got.astype(jnp.bfloat16)
+        copy(slot, base).start()
+        sent[0] = sent[0] + 1
         return carry
 
-    lax.fori_loop(0, (total + ROWS - 1) // ROWS, chunk, 0)
+    lax.fori_loop(0, (total + block - 1) // block, chunk, 0)
+
+    @pl.when(src == n_src - 1)
+    def _():
+        for back in (1, 2):
+
+            @pl.when(sent[0] >= back)
+            def _():
+                copy((sent[0] - back) & 1, 0).wait()
 
 
 def gather_rows(table, slot_rows, z_all, n_local, top_count, max_rows):
     n_src = slot_rows.shape[0]
     n_tok = z_all.shape[0] // n_src
     d_model = z_all.shape[1]
+    block = 2 * ROWS
     return pl.pallas_call(
         functools.partial(gather_kernel, n_src, n_local, top_count),
-        out_shape=jax.ShapeDtypeStruct((n_src, max_rows, d_model), jnp.bfloat16),
+        out_shape=jax.ShapeDtypeStruct((n_src, -(-max_rows // block) * block, d_model), jnp.bfloat16),
         grid_spec=pltpu.PrefetchScalarGridSpec(
             num_scalar_prefetch=1,
             grid=(n_src,),
@@ -101,10 +180,11 @@
                 pl.BlockSpec((1, 8, n_tok), lambda s, t: (s, 0, 0)),
                 pl.BlockSpec((n_tok, d_model), lambda s, t: (s, 0)),
             ],
-            out_specs=pl.BlockSpec((1, max_rows, d_model), lambda s, t: (s, 0, 0)),
+            out_specs=pl.BlockSpec(memory_space=pl.ANY),
+            scratch_shapes=[pltpu.VMEM((2, block, d_model), jnp.bfloat16), pltpu.SemaphoreType.DMA((2,)), pltpu.SMEM((1,), jnp.int32)],
         ),
         compiler_params=pltpu.CompilerParams(dimension_semantics=("arbitrary",), vmem_limit_bytes=VMEM_LIMIT),
-        cost_estimate=pl.CostEstimate(flops=2 * 6656 * n_tok * d_model, bytes_accessed=60_000_000, transcendentals=0),
+        cost_estimate=pl.CostEstimate(flops=2 * 1024 * n_src * n_tok * d_model, bytes_accessed=6 * n_src * n_tok * d_model, transcendentals=0),
         name="gather_rows",
     )(table, slot_rows, z_all)
 
@@ -112,33 +192,20 @@
 def expert_kernel(n_src, n_local, table_ref, x_hbm, ga, ua, da, gb, ub, db, y_hbm, x_buf, y_buf, in_sems, out_sems):
     step = pl.program_id(0)
     n_seg = n_src * n_local
-    bits = in_sems.shape[2]
 
     def pieces(which, act):
         slot = lax.rem(which, 2)
         for s in range(n_src):
-            off = table_ref[s * n_local + which]
-            size = table_ref[n_seg + s * n_local + which]
-            place = table_ref[2 * n_seg + s * n_local + which]
-            units = size // SEG
-            done = 0
-            for b in reversed(range(bits)):
-                length = SEG << b
-                at_hbm = pl.multiple_of(off + done, SEG)
-                at_buf = pl.multiple_of(place + done, SEG)
-                has = (units >> b) & 1
-
-                @pl.when(has == 1)
-                def _():
-                    act(slot, s, b, at_hbm, at_buf, length)
-
-                done = done + has * length
-
-    def in_copy(slot, s, b, at_hbm, at_buf, length):
-        return pltpu.make_async_copy(x_hbm.at[s, pl.ds(at_hbm, length)], x_buf.at[slot, pl.ds(at_buf, length)], in_sems.at[slot, s, b])
-
-    def out_copy(slot, s, b, at_hbm, at_buf, length):
-        return pltpu.make_async_copy(y_buf.at[slot, pl.ds(at_buf, length)], y_hbm.at[s, pl.ds(at_hbm, length)], out_sems.at[slot, s, b])
+            off = pl.multiple_of(table_ref[s * n_local + which], SEG)
+            size = pl.multiple_of(table_ref[n_seg + s * n_local + which], SEG)
+            place = pl.multiple_of(table_ref[2 * n_seg + s * n_local + which], SEG)
+            act(slot, s, off, place, size)
+
+    def in_copy(slot, s, off, place, size):
+        return pltpu.make_async_copy(x_hbm.at[s, pl.ds(off, size)], x_buf.at[slot, pl.ds(place, size)], in_sems.at[slot, s])
+
+    def out_copy(slot, s, off, place, size):
+        return pltpu.make_async_copy(y_buf.at[slot, pl.ds(place, size)], y_hbm.at[s, pl.ds(off, size)], out_sems.at[slot, s])
 
     @pl.when(step == 0)
     def _():
@@ -186,12 +253,10 @@
         pieces(step, lambda *a: out_copy(*a).wait())
 
 
-def expert_rows(table, x_rows, own, other, slot_cap):
-    n_src, max_rows, d_model = x_rows.shape
+def expert_rows(table, x_rows, own, other, buf_rows):
+    n_src, _, d_model = x_rows.shape
     half, _, width = own[0].shape
     n_local = 2 * half
-    buf_rows = -(-n_src * slot_cap // ROWS) * ROWS
-    bits = (slot_cap // SEG).bit_length()
     own_at = lambda l, t: (jnp.minimum(l, half - 1), 0, 0)
     other_at = lambda l, t: (jnp.maximum(l - half, 0), 0, 0)
     return pl.pallas_call(
@@ -213,8 +278,8 @@
             scratch_shapes=[
                 pltpu.VMEM((2, buf_rows, d_model), jnp.bfloat16),
                 pltpu.VMEM((2, buf_rows, d_model), jnp.bfloat16),
-                pltpu.SemaphoreType.DMA((2, n_src, bits)),
-                pltpu.SemaphoreType.DMA((2, n_src, bits)),
+                pltpu.SemaphoreType.DMA((2, n_src)),
+                pltpu.SemaphoreType.DMA((2, n_src)),
             ],
         ),
         compiler_params=pltpu.CompilerParams(dimension_semantics=("arbitrary",), vmem_limit_bytes=VMEM_LIMIT),
@@ -223,25 +288,53 @@
     )(table, x_rows, *own, *other)
 
 
-def combine_kernel(n_src, n_local, top_count, table_ref, cols_ref, y_ref, out_ref, slot_bc, weight_bc):
+def combine_kernel(n_src, n_local, top_count, table_ref, cols_ref, y_hbm, out_ref, slot_bc, weight_bc, buf, sems):
     src = pl.program_id(0)
     n_tok = out_ref.shape[0]
-    total = table_ref[3 * n_src * n_local + n_local + src]
+    at_total = 3 * n_src * n_local + n_local
+    total = table_ref[at_total + src]
+    n_chunks = (total + ROWS - 1) // ROWS
     lanes = 128
+    ahead = 2 + (src & 1)
+
+    def copy(which, c, slot):
+        return pltpu.make_async_copy(y_hbm.at[which, pl.ds(pl.multiple_of(c * ROWS, ROWS), ROWS)], buf.at[slot], sems.at[slot])
+
+    @pl.when(src == 0)
+    def _():
+        copy(src, 0, ahead).start()
+
+    @pl.when(src + 1 < n_src)
+    def _():
+        copy(src + 1, 0, 5 - ahead).start()
+
+    @pl.when(n_chunks > 1)
+    def _():
+        copy(src, 1, 1).start()
+
     for j in range(top_count):
         slot_bc[j] = jnp.broadcast_to(cols_ref[0, :, j : j + 1], (n_tok, lanes))
         weight_bc[j] = jnp.broadcast_to(cols_ref[0, :, top_count + j : top_count + j + 1], (n_tok, lanes))
     out_ref[...] = jnp.zeros_like(out_ref)
+    copy(src, 0, ahead).wait()
 
     def chunk(c, carry):
         base = c * ROWS
-        rows = pl.ds(pl.multiple_of(base, ROWS), ROWS)
-        y = y_ref[0, rows, :]
+        slot = jnp.where(c == 0, ahead, c & 1)
+
+        @pl.when(c > 0)
+        def _():
+            copy(src, c, slot).wait()
+
+        @pl.when((c > 0) & (c + 1 < n_chunks))
+        def _():
+            copy(src, c + 1, (c + 1) & 1).start()
+
+        y = buf[slot]
         y_at = lax.broadcasted_iota(jnp.int32, y.shape, 0) + base
         y = jnp.where(y_at < total, y, jnp.zeros_like(y))
-
-        def tokens(i, inner):
-            tok = pl.ds(pl.multiple_of(i * ROWS, ROWS), ROWS)
+        for i in range(n_tok // ROWS):
+            tok = slice(i * ROWS, (i + 1) * ROWS)
             parts = [[], [], []]
             for half in range(ROWS // lanes):
                 lane_at = (lax.broadcasted_iota(jnp.int32, (ROWS, lanes), 1) + (base + half * lanes)).astype(jnp.float32)
@@ -259,16 +352,13 @@
             acc = acc + jnp.dot(mid, y, preferred_element_type=jnp.float32)
             acc = acc + jnp.dot(high, y, preferred_element_type=jnp.float32)
             out_ref[tok, :] += acc
-            return inner
-
-        lax.fori_loop(0, n_tok // ROWS, tokens, 0)
         return carry
 
-    lax.fori_loop(0, (total + ROWS - 1) // ROWS, chunk, 0)
+    lax.fori_loop(0, n_chunks, chunk, 0)
 
 
 def combine_rows(table, cols, y_rows, n_local, top_count):
-    n_src, max_rows, d_model = y_rows.shape
+    n_src, _, d_model = y_rows.shape
     n_tok = cols.shape[1]
     return pl.pallas_call(
         functools.partial(combine_kernel, n_src, n_local, top_count),
@@ -278,18 +368,25 @@
             grid=(n_src,),
             in_specs=[
                 pl.BlockSpec((1, n_tok, 2 * top_count), lambda s, t: (s, 0, 0)),
-                pl.BlockSpec((1, max_rows, d_model), lambda s, t: (s, 0, 0)),
+                pl.BlockSpec(memory_space=pl.ANY),
             ],
             out_specs=pl.BlockSpec((n_tok, d_model), lambda s, t: (s, 0)),
             scratch_shapes=[
                 pltpu.VMEM((top_count, n_tok, 128), jnp.float32),
                 pltpu.VMEM((top_count, n_tok, 128), jnp.float32),
+                pltpu.VMEM((4, ROWS, d_model), jnp.bfloat16),
+                pltpu.SemaphoreType.DMA((4,)),
             ],
         ),
         compiler_params=pltpu.CompilerParams(dimension_semantics=("arbitrary",), vmem_limit_bytes=VMEM_LIMIT),
-        cost_estimate=pl.CostEstimate(flops=6 * 7168 * n_tok * d_model, bytes_accessed=62_000_000, transcendentals=0),
+        cost_estimate=pl.CostEstimate(flops=6 * 1024 * n_src * n_tok * d_model, bytes_accessed=8 * n_src * n_tok * d_model, transcendentals=0),
         name="combine_rows",
     )(table, cols, y_rows)
+
+
+def unit_list(n_micro, n_seq):
+    units = [(0, q, 1) for q in range(n_seq)]
+    return units + [(micro, 0, n_seq) for micro in range(1, n_micro)]
 
 
 def solution(mesh):
@@ -320,30 +417,42 @@
         from_own = ids - half * me
         from_other = ids - half * (me ^ 1)
         local_ids = jnp.where((from_own >= 0) & (from_own < half), from_own, jnp.where((from_other >= 0) & (from_other < half), from_other + half, -1))
-        plans = [route_tables(local_ids[:, m], all_weights[:, m], n_local) for m in range(n_micro)]
-
-        residuals, normeds, gathered = [], [], []
-        for m in range(n_micro):
-            residual = attention_block(tokens[m], attn_norm, w_query, w_key, w_value, w_out).reshape(n_tok, d_model)
-            normed = rms_norm(residual, ffn_norm)
-            residuals.append(residual)
-            normeds.append(normed)
-            gathered.append(lax.all_gather(normed, "ep", axis=0, tiled=True, axis_index_groups=ring_groups))
-        outs = []
-        for m in range(n_micro):
-            table, slot_rows, cols = plans[m]
-            x_rows = gather_rows(table, slot_rows, gathered[m], n_local, top_count, max_rows)
-            y_rows = expert_rows(table, x_rows, own, other, slot_cap)
+
+        gains = (attn_norm.reshape(1, d_model), ffn_norm.reshape(1, d_model))
+        attn_weights = (w_query.transpose(1, 0, 2), w_key.transpose(1, 0, 2), w_value.transpose(1, 0, 2), w_out)
+        units = unit_list(n_micro, n_seq)
+        hs, zs, gathered, plans = [], [], [], []
+        for micro, first, count in units:
+            if zs:
+                tokens, _ = lax.optimization_barrier((tokens, zs[-1]))
+            h, z = attention_rows(tokens, micro, first, count, gains, attn_weights)
+            h, z = (v.reshape(count * seq_len, d_model) for v in (h, z))
+            hs.append(h)
+            zs.append(z)
+            gathered.append(lax.all_gather(z, "ep", axis=0, tiled=True, axis_index_groups=ring_groups))
+            by_seq = lambda v: v[:, micro].reshape(n_src, top_count, n_seq, seq_len)[:, :, first : first + count].transpose(0, 2, 1, 3).reshape(n_src * count, top_count, seq_len)
+            plans.append(route_tables(by_seq(local_ids), by_seq(all_weights), n_local))
+        routed, partial = [], None
+        for k, (table, slot_rows, cols) in enumerate(plans):
+            if partial is not None:
+                table, _ = lax.optimization_barrier((table, partial))
+            x_rows = gather_rows(table, slot_rows, gathered[k], n_local, top_count, max_rows)
+            seg_rows = min(slot_cap, seq_len) * n_src * units[k][2] if units[k][2] == 1 else (slot_cap + SEG * units[k][2]) * n_src
+            y_rows = expert_rows(table, x_rows, own, other, -(-seg_rows // ROWS) * ROWS)
             partial = combine_rows(table, cols, y_rows, n_local, top_count)
-            routed = lax.psum_scatter(partial, "ep", scatter_dimension=0, tiled=True, axis_index_groups=ring_groups)
-            shared_out = swiglu(normeds[m], shared_gate, shared_up, shared_down)
-            layer_rows = residuals[m].astype(jnp.float32) + shared_out.astype(jnp.float32) + routed
-            outs.append(layer_rows.astype(jnp.bfloat16).reshape(n_seq, seq_len, d_model))
-        return jnp.stack(outs)
+            routed.append(lax.psum_scatter(partial, "ep", scatter_dimension=0, tiled=True, axis_index_groups=ring_groups))
+        outs = [[] for _ in range(n_micro)]
+        for k, (micro, first, count) in enumerate(units):
+            z = zs[k]
+            shared_out = swiglu(z, shared_gate, shared_up, shared_down)
+            layer_rows = hs[k].astype(jnp.float32) + shared_out.astype(jnp.float32) + routed[k]
+            outs[micro].append(layer_rows.astype(jnp.bfloat16).reshape(count, seq_len, d_model))
+        return jnp.stack([jnp.concatenate(parts, axis=0) if len(parts) > 1 else parts[0] for parts in outs])
 
     token_spec = P(None, ("dp", "ep"), None, None)
     route_spec = P(None, ("dp", "ep"), None)
     rep_spec = P()
     expert_spec = P("ep", None, None)
     in_specs = (token_spec, route_spec, route_spec, rep_spec, rep_spec, rep_spec, rep_spec, rep_spec, rep_spec, expert_spec, expert_spec, expert_spec, rep_spec, rep_spec, rep_spec)
+
     return jax.shard_map(device_step, mesh=mesh, in_specs=in_specs, out_specs=token_spec, check_vma=False)

time: 1010 us -> 792 us (0.78)
  matrix products: 142 us -> 43.7 us
  waiting for transfers between devices: 291 us -> 198 us
  other arithmetic: 100 us -> 32.4 us
  Pallas kernels: 441 us -> 469 us
    pallas_call x0 -> x3, Pallas kernels: none -> 119 us  [attention_rows(): pl.pallas_call(attention_kernel, out_shape=(out, out), grid=(n_heads // p...]
    dot_general x8 -> x0, matrix products: 103 us -> none  [the longest x2 33.4 us: attention_block(): jnp.einsum('...qhe,...khe->...hqk', queries, key_rows, preferred_element_...]
    all_gather x2 -> x3, waiting for transfers between devices: 97.7 us -> 0.01 us  [device_step(): lax.all_gather(z, 'ep', axis=0, tiled=True, axis_index_groups=ring_groups)]
    pallas_call x2 -> x3, Pallas kernels: 227 us -> 133 us  [combine_rows(): pl.pallas_call(functools.partial(combine_kernel, n_src, n_local, top_coun...]
    sub x2 -> x0, other arithmetic: 57.6 us -> none  [attention_block(): jax.nn.softmax(jnp.where(causal, scores, -jnp.inf), axis=-1)]
    pallas_call x2 -> x3, Pallas kernels: 124 us -> 162 us  [expert_rows(): pl.pallas_call(functools.partial(expert_kernel, n_src, n_local), out_shap...]
    pallas_call x2 -> x3, Pallas kernels: 89.7 us -> 55.3 us  [gather_rows(): pl.pallas_call(functools.partial(gather_kernel, n_src, n_local, top_count...]
    ppermute x3, waiting for transfers between devices: 0.01 us -> 29.3 us  [device_step(): other = tuple((lax.ppermute(w, 'ep', pair_perm) for w in own))]
  transfers between devices with their start and end apart: 8 -> 10, of which waited for: 2 -> 3; matrix products, arithmetic and copies ran while one was open for 25% -> 11% of each run, Pallas kernels for 44% -> 60%
where the time goes in v2:
time: 792 us; the launch traced here: 783 us
  Pallas kernels  469 us (59%)
  waiting for transfers between devices  198 us (25%)
  matrix products  43.7 us (6%)
  other arithmetic  32.4 us (4%)
  local copies, waits for them, and re-layouts  24.4 us (3%)
  between operations  14.2 us (2%)
    reduce_scatter x3, waiting for transfers between devices, device_step(): lax.psum_scatter(partial, 'ep', scatter_dimension=0, tiled=True, axis_ind...  168 us
    pallas_call x3, Pallas kernels, expert_rows(): pl.pallas_call(functools.partial(expert_kernel, n_src, n_local), out_shap...  162 us
    pallas_call x3, Pallas kernels, combine_rows(): pl.pallas_call(functools.partial(combine_kernel, n_src, n_local, top_coun...  133 us
    pallas_call x3, Pallas kernels, attention_rows(): pl.pallas_call(attention_kernel, out_shape=(out, out), grid=(n_heads // p...  119 us
    pallas_call x3, Pallas kernels, gather_rows(): pl.pallas_call(functools.partial(gather_kernel, n_src, n_local, top_count...  55.3 us
    dot_general x3, matrix products, swiglu(): jnp.dot(hidden, down_w, preferred_element_type=jnp.float32)  29.7 us
    ppermute x3, waiting for transfers between devices, device_step(): other = tuple((lax.ppermute(w, 'ep', pair_perm) for w in own))  29.3 us
  transfers between devices with their start and end apart: 10, of which 3 were waited for; matrix products, arithmetic and copies ran while one was open for 11% of the time, Pallas kernels for 60%

profile of v2, /device:TPU:112, one launch (start us, length us, event | category | flops | bytes accessed | tf_op | source)
XLA Modules:
  0.0 783.3 jit_solution(16603979880842359359)
XLA Ops:
  11.7 30.4 %attention_rows.3 = (bf16[1,512,1536]{2,1,0:T(8,128)(2,1)}, bf16[1,512,1536]{2,1,0:T(8,128)(2,1)}) custom-call(bf16[1,1536]{1,0:T(2,128)(2,1)} %reshape.220.gain_ref, bf16[1,1536]{1,0:T(2,128)(2,1)} %reshape.221.ffn_gain_ref, bf16[2,2,512,1536]{3,2,1,0:T(8,128)(2,1)} %x_ref.3, bf16[12,1536,128]{2,1,0:T(8,128)(2,1)} %bitcast.175, ...), custom_call_target="tpu_custom_call" | custom-call | flops 9663676416 | bytes 30000000 | tf_op jit(solution)/shard_map/attention_rows/pallas_call | solution.py:82
  42.2 30.4 %attention_rows.4 = (bf16[1,512,1536]{2,1,0:T(8,128)(2,1)}, bf16[1,512,1536]{2,1,0:T(8,128)(2,1)}) custom-call(bf16[1,1536]{1,0:T(2,128)(2,1)} %reshape.220.gain_ref, bf16[1,1536]{1,0:T(2,128)(2,1)} %reshape.221.ffn_gain_ref, bf16[2,2,512,1536]{3,2,1,0:T(8,128)(2,1)} %x_ref.3, bf16[12,1536,128]{2,1,0:T(8,128)(2,1)} %bitcast.176, ...), custom_call_target="tpu_custom_call" | custom-call | flops 9663676416 | bytes 30000000 | tf_op jit(solution)/shard_map/attention_rows/pallas_call | solution.py:82
  73.0 58.1 %attention_rows.5 = (bf16[2,512,1536]{2,1,0:T(8,128)(2,1)}, bf16[2,512,1536]{2,1,0:T(8,128)(2,1)}) custom-call(bf16[1,1536]{1,0:T(2,128)(2,1)} %reshape.220.gain_ref, bf16[1,1536]{1,0:T(2,128)(2,1)} %reshape.221.ffn_gain_ref, bf16[2,2,512,1536]{3,2,1,0:T(8,128)(2,1)} %x_ref.3, bf16[12,1536,128]{2,1,0:T(8,128)(2,1)} %bitcast.177, ...), custom_call_target="tpu_custom_call" | custom-call | flops 19327352832 | bytes 30000000 | tf_op jit(solution)/shard_map/attention_rows/pallas_call | solution.py:82
  142.9 14.6 %gather_rows.3.x_hbm = bf16[4,3072,1536]{2,1,0:T(8,128)(2,1)} custom-call(s32[212]{0:T(256)} %concatenate.34.table_ref, s32[4,8,512]{2,1,0:T(8,128)} %concatenate.36.clone.slots_ref, bf16[2048,1536]{1,0:T(8,128)(2,1)} %bitcast.149), custom_call_target="tpu_custom_call" | custom-call | flops 6442450944 | bytes 18874368 | tf_op jit(solution)/shard_map/gather_rows/pallas_call | solution.py:173
  157.5 11.3 %collective-permute-done.1.ub = bf16[8,1536,512]{2,1,0:T(8,128)(2,1)} collective-permute-done((bf16[8,1536,512]{2,1,0:T(8,128)(2,1)}, bf16[8,1536,512]{2,1,0:T(8,128)(2,1)}, u32[]{:S(2)}, u32[]{:S(2)}) %collective-permute-start.1) | collective-permute-done | bytes 12582944 | tf_op jit(solution)/shard_map/ppermute | solution.py:409
  168.8 18.0 %collective-permute-done.2.db = bf16[8,512,1536]{2,1,0:T(8,128)(2,1)} collective-permute-done((bf16[8,512,1536]{2,1,0:T(8,128)(2,1)}, bf16[8,512,1536]{2,1,0:T(8,128)(2,1)}, u32[]{:S(2)}, u32[]{:S(2)}) %collective-permute-start.2) | collective-permute-done | bytes 12582944 | tf_op jit(solution)/shard_map/ppermute | solution.py:409
  186.7 48.2 %expert_rows.3.y_hbm = bf16[4,3072,1536]{2,1,0:T(8,128)(2,1)} custom-call(s32[212]{0:T(256)} %concatenate.34.table_ref, bf16[4,3072,1536]{2,1,0:T(8,128)(2,1)} %gather_rows.3.x_hbm, bf16[8,1536,512]{2,1,0:T(8,128)(2,1)} %ga.5, bf16[8,1536,512]{2,1,0:T(8,128)(2,1)} %ua.5, bf16[8,512,1536]{2,1,0:T(8,128)(2,1)} %da.5, ...), custom_call_target="tpu_custom_call" | custom-call | flops 38654705664 | bytes 115000000 | tf_op jit(solution)/shard_map/expert_rows/pallas_call | solution.py:262
  235.0 34.2 %combine_rows.3 = f32[2048,1536]{1,0:T(8,128)} custom-call(s32[212]{0:T(256)} %concatenate.34.table_ref, f32[4,512,12]{2,1,0:T(8,128)} %maximum_bitcast_fusion.2.cols_ref, bf16[4,3072,1536]{2,1,0:T(8,128)(2,1)} %expert_rows.3.y_hbm), custom_call_target="tpu_custom_call" | custom-call | flops 19327352832 | bytes 25165824 | tf_op jit(solution)/shard_map/combine_rows/pallas_call | solution.py:363
  275.9 14.5 %gather_rows.4.x_hbm = bf16[4,3072,1536]{2,1,0:T(8,128)(2,1)} custom-call(s32[212]{0:T(256)} %concatenate.37.table_ref, s32[4,8,512]{2,1,0:T(8,128)} %concatenate.39.clone.slots_ref, bf16[2048,1536]{1,0:T(8,128)(2,1)} %bitcast.148), custom_call_target="tpu_custom_call" | custom-call | flops 6442450944 | bytes 18874368 | tf_op jit(solution)/shard_map/gather_rows/pallas_call | solution.py:173
  290.5 47.6 %expert_rows.4.y_hbm = bf16[4,3072,1536]{2,1,0:T(8,128)(2,1)} custom-call(s32[212]{0:T(256)} %concatenate.37.table_ref, bf16[4,3072,1536]{2,1,0:T(8,128)(2,1)} %gather_rows.4.x_hbm, bf16[8,1536,512]{2,1,0:T(8,128)(2,1)} %ga.5, bf16[8,1536,512]{2,1,0:T(8,128)(2,1)} %ua.5, bf16[8,512,1536]{2,1,0:T(8,128)(2,1)} %da.5, ...), custom_call_target="tpu_custom_call" | custom-call | flops 38654705664 | bytes 115000000 | tf_op jit(solution)/shard_map/expert_rows/pallas_call | solution.py:262
  338.1 34.4 %combine_rows.4 = f32[2048,1536]{1,0:T(8,128)} custom-call(s32[212]{0:T(256)} %concatenate.37.table_ref, f32[4,512,12]{2,1,0:T(8,128)} %maximum_bitcast_fusion.3.cols_ref, bf16[4,3072,1536]{2,1,0:T(8,128)(2,1)} %expert_rows.4.y_hbm), custom_call_target="tpu_custom_call" | custom-call | flops 19327352832 | bytes 25165824 | tf_op jit(solution)/shard_map/combine_rows/pallas_call | solution.py:363
  379.2 3.4 broadcast_add_fusion
  386.2 3.5 maximum_bitcast_fusion.1.cols_ref
  389.7 26.3 %gather_rows.5.x_hbm = bf16[8,3072,1536]{2,1,0:T(8,128)(2,1)} custom-call(s32[408]{0:T(512)} %concatenate.41.table_ref, s32[8,8,512]{2,1,0:T(8,128)} %concatenate.43.clone.slots_ref, bf16[4096,1536]{1,0:T(8,128)(2,1)} %all-gather.9.cloned.1.call-done.z_ref), custom_call_target="tpu_custom_call" | custom-call | flops 12884901888 | bytes 37748736 | tf_op jit(solution)/shard_map/gather_rows/pallas_call | solution.py:173
  415.9 66.5 %expert_rows.5.y_hbm = bf16[8,3072,1536]{2,1,0:T(8,128)(2,1)} custom-call(s32[408]{0:T(512)} %concatenate.41.table_ref, bf16[8,3072,1536]{2,1,0:T(8,128)(2,1)} %gather_rows.5.x_hbm, bf16[8,1536,512]{2,1,0:T(8,128)(2,1)} %ga.5, bf16[8,1536,512]{2,1,0:T(8,128)(2,1)} %ua.5, bf16[8,512,1536]{2,1,0:T(8,128)(2,1)} %da.5, ...), custom_call_target="tpu_custom_call" | custom-call | flops 38654705664 | bytes 115000000 | tf_op jit(solution)/shard_map/expert_rows/pallas_call | solution.py:262
  482.5 64.1 %combine_rows.5 = f32[4096,1536]{1,0:T(8,128)} custom-call(s32[408]{0:T(512)} %concatenate.41.table_ref, f32[8,512,12]{2,1,0:T(8,128)} %maximum_bitcast_fusion.1.cols_ref, bf16[8,3072,1536]{2,1,0:T(8,128)(2,1)} %expert_rows.5.y_hbm), custom_call_target="tpu_custom_call" | custom-call | flops 38654705664 | bytes 50331648 | tf_op jit(solution)/shard_map/combine_rows/pallas_call | solution.py:363
  548.0 5.2 fusion.44
  556.4 5.1 fusion.66
  561.4 8.6 %convolution_convert_fusion.1 = bf16[512,1536]{1,0:T(8,128)(2,1)} fusion(bf16[1024,1536]{1,0:T(8,128)(2,1)} %param.29, f32[512,1024]{1,0:T(8,128)} %fusion.44, bf16[1536,1024]{1,0:T(8,128)(2,1)} %param.28, bf16[1,512,1536]{2,1,0:T(8,128)(2,1)} %get-tuple-element.19), kind=kOutput, calls=%fused_computation.13 | convolution fusion | flops 3225157632 | bytes 11534336 | tf_op jit(solution)/shard_map/dot_general | solution.py:99
  570.0 8.6 %convolution_convert_fusion.2 = bf16[512,1536]{1,0:T(8,128)(2,1)} fusion(bf16[1024,1536]{1,0:T(8,128)(2,1)} %param.29, f32[512,1024]{1,0:T(8,128)} %fusion.48, bf16[1536,1024]{1,0:T(8,128)(2,1)} %param.28, bf16[1,512,1536]{2,1,0:T(8,128)(2,1)} %get-tuple-element.16), kind=kOutput, calls=%fused_computation.14 | convolution fusion | flops 3225157632 | bytes 11534336 | tf_op jit(solution)/shard_map/dot_general | solution.py:99
  578.5 12.5 %convolution_convert_fusion = bf16[1024,1536]{1,0:T(8,128)(2,1)} fusion(bf16[1024,1536]{1,0:T(8,128)(2,1)} %param.29, f32[1024,1024]{1,0:T(8,128)} %fusion.66, bf16[1024,1536]{1,0:T(8,128)(2,1)S(1)} %bitcast.154, bf16[1536,1024]{1,0:T(8,128)(2,1)} %param.28), kind=kOutput, calls=%fused_computation.5 | convolution fusion | flops 6450315264 | bytes 16777216 | tf_op jit(solution)/shard_map/dot_general | solution.py:99
  591.1 4.7 fusion.6
  598.8 168.3 %reduce-scatter.8.cloned.1.call-done = f32[1024,1536]{1,0:T(8,128)} async-done(((f32[4096,1536]{1,0:T(8,128)}), f32[1024,1536]{1,0:T(8,128)}) %reduce-scatter.8.cloned.1.call-update) | async-done | bytes 6291472 | tf_op jit(solution)/shard_map/reduce_scatter | solution.py:443
  767.1 5.9 fusion.1
  (130 shorter events, 44.9 us)
Async XLA Ops:
  6.5 125.4 %all-gather.7.cloned.1.call-start = ((), (), s32[]{:S(2)}) async-start(), calls=%async_computation.3 | async-start | bytes 1179648 | tf_op jit(solution)/shard_map/all_gather | solution.py:412
  9.1 133.8 %all-gather.11.cloned.1.call-start = ((), (), s32[]{:S(2)}) async-start(), calls=%async_computation.8 | async-start | bytes 7864320 | tf_op jit(solution)/shard_map/all_gather | solution.py:432
  42.2 233.8 %all-gather.13.cloned.1.call-start = ((), (), s32[]{:S(2)}) async-start(), calls=%async_computation.9 | async-start | bytes 7864320 | tf_op jit(solution)/shard_map/all_gather | solution.py:432
  72.7 316.9 %all-gather.9.cloned.1.call-start = ((), (), s32[]{:S(2)}) async-start(), calls=%async_computation.6 | async-start | bytes 15728640 | tf_op jit(solution)/shard_map/all_gather | solution.py:432
  131.1 460.0 %reduce-scatter.4.cloned.1.call-start = ((), (), s32[]{:S(2)}) async-start(), calls=%async_computation.4 | async-start | bytes 15728640 | tf_op jit(solution)/shard_map/reduce_scatter | solution.py:443
  131.2 26.3 %collective-permute-start = (bf16[8,1536,512]{2,1,0:T(8,128)(2,1)}, bf16[8,1536,512]{2,1,0:T(8,128)(2,1)}, u32[]{:S(2)}, u32[]{:S(2)}) collective-permute-start(bf16[8,1536,512]{2,1,0:T(8,128)(2,1)} %ga.5), channel_id=1, source_target_pairs={{0,1},{1,0},{2,3},{3,2},{4,5},{5,4},{6,7},{7,6},{8,9},{9,8},{10,11... | collective-permute-start | bytes 37748744 | tf_op jit(solution)/shard_map/ppermute | solution.py:409
  131.3 37.5 %collective-permute-start.1 = (bf16[8,1536,512]{2,1,0:T(8,128)(2,1)}, bf16[8,1536,512]{2,1,0:T(8,128)(2,1)}, u32[]{:S(2)}, u32[]{:S(2)}) collective-permute-start(bf16[8,1536,512]{2,1,0:T(8,128)(2,1)} %ua.5), channel_id=1, source_target_pairs={{0,1},{1,0},{2,3},{3,2},{4,5},{5,4},{6,7},{7,6},{8,9},{9,8},{10,11... | collective-permute-start | bytes 37748744 | tf_op jit(solution)/shard_map/ppermute | solution.py:409
  131.8 55.0 %collective-permute-start.2 = (bf16[8,512,1536]{2,1,0:T(8,128)(2,1)}, bf16[8,512,1536]{2,1,0:T(8,128)(2,1)}, u32[]{:S(2)}, u32[]{:S(2)}) collective-permute-start(bf16[8,512,1536]{2,1,0:T(8,128)(2,1)} %da.5), channel_id=1, source_target_pairs={{0,1},{1,0},{2,3},{3,2},{4,5},{5,4},{6,7},{7,6},{8,9},{9,8},{10,11... | collective-permute-start | bytes 37748744 | tf_op jit(solution)/shard_map/ppermute | solution.py:409
  131.9 5.2 copy-start.8
  269.2 326.6 %reduce-scatter.6.cloned.1.call-start = ((), (), s32[]{:S(2)}) async-start(), calls=%async_computation.5 | async-start | bytes 15728640 | tf_op jit(solution)/shard_map/reduce_scatter | solution.py:443
  372.4 0.9 copy-start.7
  372.5 1.0 copy-start.6
  372.5 2.2 copy-start.9
  372.5 394.6 %reduce-scatter.8.cloned.1.call-start = ((), (), s32[]{:S(2)}) async-start(), calls=%async_computation.7 | async-start | bytes 31457280 | tf_op jit(solution)/shard_map/reduce_scatter | solution.py:443
  546.6 1.4 copy-start.3
  548.0 5.2 copy-start.2
  548.0 5.2 copy-start.10
  553.2 3.2 copy-start.1
  591.1 4.8 copy-start.4
  591.1 4.8 copy-start.5
  595.8 2.6 copy-start
Sparse Core Ops, SparseCore 0:
  9.2 22.0 all-gather.6
  42.3 64.4 all-gather.10
  108.3 62.1 all-gather.12
  171.9 115.1 all-gather.8
  289.3 111.3 reduce-scatter.3
  402.9 110.1 reduce-scatter.5
  546.8 220.2 reduce-scatter.7

commit v3 on v2

--- a/solution.py
+++ b/solution.py
@@ -13,6 +13,10 @@
 SLOT_ALIGN = 8
 SEG = 16
 ROWS = 256
+Q_BLOCKS = 1
+FIELD = 128
+PIECE = 8 * FIELD
+BY_HOPS = True
 VMEM_LIMIT = 64_000_000
 
 
@@ -30,7 +34,7 @@
     group, seq = pl.program_id(0), pl.program_id(1)
     seq_len, d_model = normed.shape[1:]
     per, _, head_dim = wq_ref.shape
-    block = seq_len // 2
+    block = seq_len // Q_BLOCKS
 
     @pl.when(group == 0)
     def _():
@@ -40,19 +44,21 @@
     project = lambda w_ref: jnp.dot(rows, jnp.concatenate([w_ref[i] for i in range(per)], axis=1), preferred_element_type=jnp.float32).astype(jnp.bfloat16)
     queries, key_rows, value_rows = project(wq_ref), project(wk_ref), project(wv_ref)
     above = lax.broadcasted_iota(jnp.int32, (block, block), 0) < lax.broadcasted_iota(jnp.int32, (block, block), 1)
-    tops, ends = [], []
+    heads = []
     for i in range(per):
         lanes = slice(i * head_dim, (i + 1) * head_dim)
         k, v = key_rows[:, lanes], value_rows[:, lanes]
-        for part, outs in ((0, tops), (1, ends)):
+        outs = []
+        for part in range(Q_BLOCKS):
             q = queries[part * block : (part + 1) * block, lanes]
             scores = lax.dot_general(q, k[: (part + 1) * block], (((1,), (1,)), ((), ())), preferred_element_type=jnp.float32) * (head_dim**-0.5)
             diag = jnp.where(above, -jnp.inf, scores[:, part * block :])
-            scores = diag if part == 0 else jnp.concatenate([scores[:, :block], diag], axis=1)
+            scores = diag if part == 0 else jnp.concatenate([scores[:, : part * block], diag], axis=1)
             shifted = jnp.exp(scores - jnp.max(scores, axis=1, keepdims=True))
             probs = (shifted * (1.0 / jnp.sum(shifted, axis=1, keepdims=True))).astype(jnp.bfloat16)
             outs.append(jnp.dot(probs, v[: (part + 1) * block], preferred_element_type=jnp.float32).astype(jnp.bfloat16))
-    mix = jnp.concatenate([jnp.concatenate(tops, axis=1), jnp.concatenate(ends, axis=1)], axis=0)
+        heads.append(jnp.concatenate(outs, axis=0))
+    mix = jnp.concatenate(heads, axis=1)
     added = jnp.dot(mix, wo_ref[...].reshape(per * head_dim, d_model), preferred_element_type=jnp.float32)
 
     @pl.when(group == 0)
@@ -73,7 +79,7 @@
 def attention_rows(tokens, micro, first, n_seq, gains, weights):
     _, _, seq_len, d_model = tokens.shape
     n_heads, _, head_dim = weights[0].shape
-    per = 2
+    per = 4 if n_heads % 4 == 0 else 1
     out = jax.ShapeDtypeStruct((n_seq, seq_len, d_model), jnp.bfloat16)
     whole = pl.BlockSpec((n_seq, seq_len, d_model), lambda g, s: (0, 0, 0))
     gain = pl.BlockSpec((1, d_model), lambda g, s: (0, 0))
@@ -99,33 +105,122 @@
     return jnp.dot(hidden, down_w, preferred_element_type=jnp.float32).astype(jnp.bfloat16)
 
 
-def route_tables(local_ids, weights, n_local):
-    n_src, _, n_tok = local_ids.shape
-    hits = local_ids[:, :, None, :] == jnp.arange(n_local)[None, None, :, None]
-    mask = jnp.any(hits, axis=1)
-    upper = (jnp.arange(n_tok)[:, None] <= jnp.arange(n_tok)[None, :]).astype(jnp.bfloat16)
-    running = jnp.dot(mask.astype(jnp.bfloat16).reshape(n_src * n_local, n_tok), upper, preferred_element_type=jnp.float32)
-    running = running.astype(jnp.int32).reshape(n_src, n_local, n_tok)
-    counts = running[:, :, -1]
-    padded = (counts + SEG - 1) // SEG * SEG
-    before_e = (jnp.arange(n_local)[:, None] < jnp.arange(n_local)[None, :]).astype(jnp.int32)
-    before_s = (jnp.arange(n_src)[:, None] < jnp.arange(n_src)[None, :]).astype(jnp.int32)
-    offs = jnp.sum(padded[:, :, None] * before_e[None], axis=1)
-    places = jnp.sum(padded[:, None, :] * before_s[:, :, None], axis=0)
-    slot_of = offs[:, :, None] + running - 1
-    slots = jnp.sum(jnp.where(hits, slot_of[:, None] + 1, 0), axis=2) - 1
-    table = jnp.concatenate([offs.reshape(-1), padded.reshape(-1), places.reshape(-1), jnp.sum(padded, axis=0), jnp.sum(padded, axis=1)])
-    pad_rows = jnp.full((n_src, 8 - slots.shape[1], n_tok), -1, jnp.int32)
-    slot_rows = jnp.concatenate([slots, pad_rows], axis=1)
-    cols = jnp.concatenate([slots.astype(jnp.float32), weights], axis=1).transpose(0, 2, 1)
-    return table, slot_rows, cols
-
-
-def gather_kernel(n_src, n_local, top_count, table_ref, slots_ref, z_ref, x_hbm, buf, sems, sent):
+def route_kernel(half, top_count, me_ref, meta_ref, slots_ref, cols_ref, table_ref, upper, placed):
+    micro, src, seq = (pl.program_id(i) for i in range(3))
+    me = me_ref[0]
+    n_local, n_tok = 2 * half, upper.shape[0]
+    acc = jnp.where(micro == 0, seq, 0)
+
+    @pl.when((micro == 0) & (src == 0) & (seq == 0))
+    def _():
+        below = lax.broadcasted_iota(jnp.int32, upper.shape, 0) <= lax.broadcasted_iota(jnp.int32, upper.shape, 1)
+        upper[...] = jnp.where(below, 1.0, 0.0).astype(jnp.bfloat16)
+
+    @pl.when((src == 0) & ((micro == 0) | (seq == 0)))
+    def _():
+        placed[acc] = jnp.zeros(placed.shape[1:], jnp.float32)
+
+    ids = meta_ref[0:top_count, :].astype(jnp.int32)
+    from_own, from_other = ids - half * me, ids - half * (me ^ 1)
+    local = jnp.where((from_own >= 0) & (from_own < half), from_own, jnp.where((from_other >= 0) & (from_other < half), from_other + half, -1))
+    expert_at = lax.broadcasted_iota(jnp.int32, (n_local, n_tok), 0)
+    hits = [local[j : j + 1, :] == expert_at for j in range(top_count)]
+    mask = jnp.where(functools.reduce(jnp.logical_or, hits), 1.0, 0.0)
+    bits = mask.astype(jnp.bfloat16)
+    running = jnp.dot(bits, upper[...], preferred_element_type=jnp.float32)
+    pad = lambda counts: jnp.floor((counts + (SEG - 1)) * (1.0 / SEG))
+    units = jnp.broadcast_to(pad(running[:, n_tok - 1 : n_tok]), (n_local, FIELD)).astype(jnp.bfloat16)
+    before = lax.broadcasted_iota(jnp.int32, (n_local, n_local), 1) < lax.broadcasted_iota(jnp.int32, (n_local, n_local), 0)
+    offs = jnp.dot(jnp.where(before, 1.0, 0.0).astype(jnp.bfloat16), units, preferred_element_type=jnp.float32) * SEG
+    row_of = offs[:, 0:1] + running
+    slots = [jnp.sum(jnp.where(hit, row_of, 0.0), axis=0, keepdims=True) - 1.0 for hit in hits]
+    none = jnp.full((1, n_tok), -1.0, jnp.float32)
+    slots_ref[...] = jnp.concatenate(slots + [none] * (8 - top_count), axis=0).astype(jnp.int32)
+    cols_ref[...] = jnp.concatenate(slots + [meta_ref[top_count : 2 * top_count, :]] + [none] * (16 - 2 * top_count), axis=0)
+    wide = jnp.concatenate([bits, jnp.zeros((FIELD - n_local, n_tok), jnp.bfloat16)], axis=0)
+    counts = lax.dot_general(jnp.ones((8, n_tok), jnp.bfloat16), wide, (((1,), (1,)), ((), ())), preferred_element_type=jnp.float32)
+    units_row = pad(counts)
+    before_row = lax.broadcasted_iota(jnp.int32, (FIELD, FIELD), 0) < lax.broadcasted_iota(jnp.int32, (FIELD, FIELD), 1)
+    offs_row = jnp.dot(units_row.astype(jnp.bfloat16), jnp.where(before_row, 1.0, 0.0).astype(jnp.bfloat16), preferred_element_type=jnp.float32) * SEG
+    sizes_row = units_row * SEG
+    at = lax.broadcasted_iota(jnp.int32, (8, FIELD), 0)
+    fields = jnp.where(at == 0, offs_row, jnp.where(at == 1, sizes_row, placed[acc]))
+    table_ref[...] = fields.astype(jnp.int32)
+    placed[acc] = placed[acc] + sizes_row
+
+
+def route_rows(meta, me, half, top_count, n_src, n_micro, n_seq, seq_len):
+    spot = lambda m, s, q, t: (m, s, q, 0, 0)
+    piece = lambda rows, lanes, dtype: (jax.ShapeDtypeStruct((n_micro, n_src, n_seq, rows, lanes), dtype), pl.BlockSpec((None, None, None, rows, lanes), spot))
+    outs = [piece(8, seq_len, jnp.int32), piece(16, seq_len, jnp.float32), piece(8, FIELD, jnp.int32)]
+    return pl.pallas_call(
+        functools.partial(route_kernel, half, top_count),
+        out_shape=tuple(o[0] for o in outs),
+        grid_spec=pltpu.PrefetchScalarGridSpec(
+            num_scalar_prefetch=1,
+            grid=(n_micro, n_src, n_seq),
+            in_specs=[pl.BlockSpec((16, seq_len), lambda m, s, q, t: ((2 * s + lax.rem(t[0], 2)) * n_micro + m, q))],
+            out_specs=tuple(o[1] for o in outs),
+            scratch_shapes=[pltpu.VMEM((seq_len, seq_len), jnp.bfloat16), pltpu.VMEM((n_seq, 8, FIELD), jnp.float32)],
+        ),
+        compiler_params=pltpu.CompilerParams(dimension_semantics=("arbitrary",) * 3),
+        cost_estimate=pl.CostEstimate(flops=500_000_000, bytes_accessed=2_000_000, transcendentals=0),
+        name="route_rows",
+    )(me, meta)
+
+
+class Unit:
+    def __init__(self, micro, first, count, n_src, n_seq):
+        self.micro, self.first, self.count, self.n_src, self.n_seq = micro, first, count, n_src, n_seq
+        self.pieces = n_src * count
+
+    def spot(self, i):
+        return self.micro, i // self.count, self.first + i % self.count
+
+    def field(self, table_ref, i, which, expert):
+        micro, src, seq = self.spot(i)
+        return table_ref[((micro * self.n_src + src) * self.n_seq + seq) * PIECE + which * FIELD + expert]
+
+    def rows_of(self, table_ref, i, n_local):
+        return self.field(table_ref, i, 0, n_local - 1) + self.field(table_ref, i, 1, n_local - 1)
+
+    def spec(self, rows, lanes):
+        return pl.BlockSpec((None, None, None, rows, lanes), lambda i, *_: (*self.spot(i), 0, 0))
+
+
+def gather_kernel(unit, n_local, top_count, table_ref, slots_ref, *refs):
+    z_refs, (x_hbm, buf, sems, sent) = refs[: -4 if len(refs) == 5 else -6], (refs[-4:] if len(refs) == 5 else refs[-6:-2])
     src = pl.program_id(0)
-    n_tok = z_ref.shape[0]
-    total = table_ref[3 * n_src * n_local + n_local + src]
+    total = unit.rows_of(table_ref, src, n_local)
     block = buf.shape[1]
+    n_tok = slots_ref.shape[1]
+    if len(refs) == 5:
+        z = z_refs[0]
+    else:
+        z_buf, z_sems = refs[-2:]
+        x_at = table_ref[table_ref.shape[0] - 1] // 2
+
+        def fetch(i):
+            _, s, q = unit.spot(i)
+            away = lax.rem(s - x_at + unit.n_src, unit.n_src)
+            own, left, right, far = z_refs[0], z_refs[1:3], z_refs[3:5], z_refs[5:7]
+            for seq in range(unit.count):
+                for hop, ref in enumerate((own.at[seq], right[seq], far[seq], left[seq])):
+
+                    @pl.when((q == seq) & (away == hop))
+                    def _():
+                        pltpu.make_async_copy(ref, z_buf.at[i & 1], z_sems.at[i & 1]).start()
+
+        @pl.when(src == 0)
+        def _():
+            fetch(src)
+
+        @pl.when(src + 1 < unit.pieces)
+        def _():
+            fetch(src + 1)
+
+        pltpu.make_async_copy(z_refs[1], z_buf.at[src & 1], z_sems.at[src & 1]).wait()
+        z = z_buf.at[src & 1]
 
     @pl.when(src == 0)
     def _():
@@ -144,11 +239,11 @@
 
         for part in range(block // ROWS):
             rows = lax.broadcasted_iota(jnp.int32, (ROWS, n_tok), 0) + (base + part * ROWS)
-            hit = rows == slots_ref[0, 0:1, :]
+            hit = rows == slots_ref[0:1, :]
             for j in range(1, top_count):
-                hit = hit | (rows == slots_ref[0, j : j + 1, :])
+                hit = hit | (rows == slots_ref[j : j + 1, :])
             pick = jnp.where(hit, 1.0, 0.0).astype(jnp.bfloat16)
-            got = jnp.dot(pick, z_ref[...], preferred_element_type=jnp.float32)
+            got = jnp.dot(pick, z[...], preferred_element_type=jnp.float32)
             buf[slot, part * ROWS : (part + 1) * ROWS, :] = got.astype(jnp.bfloat16)
         copy(slot, base).start()
         sent[0] = sent[0] + 1
@@ -156,7 +251,7 @@
 
     lax.fori_loop(0, (total + block - 1) // block, chunk, 0)
 
-    @pl.when(src == n_src - 1)
+    @pl.when(src == unit.pieces - 1)
     def _():
         for back in (1, 2):
 
@@ -165,40 +260,38 @@
                 copy((sent[0] - back) & 1, 0).wait()
 
 
-def gather_rows(table, slot_rows, z_all, n_local, top_count, max_rows):
-    n_src = slot_rows.shape[0]
-    n_tok = z_all.shape[0] // n_src
-    d_model = z_all.shape[1]
+def gather_rows(unit, table, slots, zs, n_local, top_count, max_rows):
+    n_tok = slots.shape[-1]
+    d_model = zs[0].shape[-1]
     block = 2 * ROWS
+    held = len(zs) > 1
+    z_specs = [pl.BlockSpec(memory_space=pl.ANY)] * len(zs) if held else [pl.BlockSpec((n_tok, d_model), lambda i, t: (i, 0))]
+    scratch = [pltpu.VMEM((2, block, d_model), jnp.bfloat16), pltpu.SemaphoreType.DMA((2,)), pltpu.SMEM((1,), jnp.int32)]
+    if held:
+        scratch += [pltpu.VMEM((2, n_tok, d_model), jnp.bfloat16), pltpu.SemaphoreType.DMA((2,))]
     return pl.pallas_call(
-        functools.partial(gather_kernel, n_src, n_local, top_count),
-        out_shape=jax.ShapeDtypeStruct((n_src, -(-max_rows // block) * block, d_model), jnp.bfloat16),
+        functools.partial(gather_kernel, unit, n_local, top_count),
+        out_shape=jax.ShapeDtypeStruct((unit.pieces, -(-max_rows // block) * block, d_model), jnp.bfloat16),
         grid_spec=pltpu.PrefetchScalarGridSpec(
             num_scalar_prefetch=1,
-            grid=(n_src,),
-            in_specs=[
-                pl.BlockSpec((1, 8, n_tok), lambda s, t: (s, 0, 0)),
-                pl.BlockSpec((n_tok, d_model), lambda s, t: (s, 0)),
-            ],
+            grid=(unit.pieces,),
+            in_specs=[unit.spec(8, n_tok), *z_specs],
             out_specs=pl.BlockSpec(memory_space=pl.ANY),
-            scratch_shapes=[pltpu.VMEM((2, block, d_model), jnp.bfloat16), pltpu.SemaphoreType.DMA((2,)), pltpu.SMEM((1,), jnp.int32)],
+            scratch_shapes=scratch,
         ),
         compiler_params=pltpu.CompilerParams(dimension_semantics=("arbitrary",), vmem_limit_bytes=VMEM_LIMIT),
-        cost_estimate=pl.CostEstimate(flops=2 * 1024 * n_src * n_tok * d_model, bytes_accessed=6 * n_src * n_tok * d_model, transcendentals=0),
+        cost_estimate=pl.CostEstimate(flops=2 * 1024 * unit.pieces * n_tok * d_model, bytes_accessed=6 * unit.pieces * n_tok * d_model, transcendentals=0),
         name="gather_rows",
-    )(table, slot_rows, z_all)
-
-
-def expert_kernel(n_src, n_local, table_ref, x_hbm, ga, ua, da, gb, ub, db, y_hbm, x_buf, y_buf, in_sems, out_sems):
+    )(table, slots, *zs)
+
+
+def expert_kernel(unit, n_local, table_ref, x_hbm, ga, ua, da, gb, ub, db, y_hbm, x_buf, y_buf, in_sems, out_sems):
     step = pl.program_id(0)
-    n_seg = n_src * n_local
 
     def pieces(which, act):
         slot = lax.rem(which, 2)
-        for s in range(n_src):
-            off = pl.multiple_of(table_ref[s * n_local + which], SEG)
-            size = pl.multiple_of(table_ref[n_seg + s * n_local + which], SEG)
-            place = pl.multiple_of(table_ref[2 * n_seg + s * n_local + which], SEG)
+        for s in range(unit.pieces):
+            off, size, place = (pl.multiple_of(unit.field(table_ref, s, f, which), SEG) for f in range(3))
             act(slot, s, off, place, size)
 
     def in_copy(slot, s, off, place, size):
@@ -222,7 +315,7 @@
         pieces(step - 2, lambda *a: out_copy(*a).wait())
 
     slot = lax.rem(step, 2)
-    total = table_ref[3 * n_seg + step]
+    total = unit.field(table_ref, unit.pieces - 1, 1, step) + unit.field(table_ref, unit.pieces - 1, 2, step)
     n_blocks = (total + ROWS - 1) // ROWS
 
     def run(gate, up, down):
@@ -253,14 +346,14 @@
         pieces(step, lambda *a: out_copy(*a).wait())
 
 
-def expert_rows(table, x_rows, own, other, buf_rows):
+def expert_rows(unit, table, x_rows, own, other, buf_rows):
     n_src, _, d_model = x_rows.shape
     half, _, width = own[0].shape
     n_local = 2 * half
     own_at = lambda l, t: (jnp.minimum(l, half - 1), 0, 0)
     other_at = lambda l, t: (jnp.maximum(l - half, 0), 0, 0)
     return pl.pallas_call(
-        functools.partial(expert_kernel, n_src, n_local),
+        functools.partial(expert_kernel, unit, n_local),
         out_shape=jax.ShapeDtypeStruct(x_rows.shape, jnp.bfloat16),
         grid_spec=pltpu.PrefetchScalarGridSpec(
             num_scalar_prefetch=1,
@@ -288,11 +381,11 @@
     )(table, x_rows, *own, *other)
 
 
-def combine_kernel(n_src, n_local, top_count, table_ref, cols_ref, y_hbm, out_ref, slot_bc, weight_bc, buf, sems):
+def combine_kernel(unit, n_local, top_count, table_ref, cols_ref, y_hbm, out_ref, slot_bc, weight_bc, buf, sems):
     src = pl.program_id(0)
     n_tok = out_ref.shape[0]
-    at_total = 3 * n_src * n_local + n_local
-    total = table_ref[at_total + src]
+    n_src = unit.pieces
+    total = unit.rows_of(table_ref, src, n_local)
     n_chunks = (total + ROWS - 1) // ROWS
     lanes = 128
     ahead = 2 + (src & 1)
@@ -312,9 +405,10 @@
     def _():
         copy(src, 1, 1).start()
 
+    cols = cols_ref[...].T
     for j in range(top_count):
-        slot_bc[j] = jnp.broadcast_to(cols_ref[0, :, j : j + 1], (n_tok, lanes))
-        weight_bc[j] = jnp.broadcast_to(cols_ref[0, :, top_count + j : top_count + j + 1], (n_tok, lanes))
+        slot_bc[j] = jnp.broadcast_to(cols[:, j : j + 1], (n_tok, lanes))
+        weight_bc[j] = jnp.broadcast_to(cols[:, top_count + j : top_count + j + 1], (n_tok, lanes))
     out_ref[...] = jnp.zeros_like(out_ref)
     copy(src, 0, ahead).wait()
 
@@ -357,17 +451,17 @@
     lax.fori_loop(0, n_chunks, chunk, 0)
 
 
-def combine_rows(table, cols, y_rows, n_local, top_count):
+def combine_rows(unit, table, cols, y_rows, n_local, top_count):
     n_src, _, d_model = y_rows.shape
-    n_tok = cols.shape[1]
+    n_tok = cols.shape[-1]
     return pl.pallas_call(
-        functools.partial(combine_kernel, n_src, n_local, top_count),
+        functools.partial(combine_kernel, unit, n_local, top_count),
         out_shape=jax.ShapeDtypeStruct((n_src * n_tok, d_model), jnp.float32),
         grid_spec=pltpu.PrefetchScalarGridSpec(
             num_scalar_prefetch=1,
             grid=(n_src,),
             in_specs=[
-                pl.BlockSpec((1, n_tok, 2 * top_count), lambda s, t: (s, 0, 0)),
+                unit.spec(16, n_tok),
                 pl.BlockSpec(memory_space=pl.ANY),
             ],
             out_specs=pl.BlockSpec((n_tok, d_model), lambda s, t: (s, 0)),
@@ -384,9 +478,29 @@
     )(table, cols, y_rows)
 
 
-def unit_list(n_micro, n_seq):
-    units = [(0, q, 1) for q in range(n_seq)]
-    return units + [(micro, 0, n_seq) for micro in range(1, n_micro)]
+def finish_kernel(*refs):
+    h_ref, shared_ref, routed_ref, out_ref = refs[-4:]
+    total = h_ref[...].astype(jnp.float32) + shared_ref[...].astype(jnp.float32) + routed_ref[...]
+    out_ref[...] = total.astype(jnp.bfloat16)
+
+
+def finish_rows(unit, held, h, shared, routed, shape):
+    n_micro, n_seq, seq_len, d_model = shape
+    block = seq_len // 2
+    base = (unit.micro * n_seq + unit.first) * 2
+    rows = pl.BlockSpec((block, d_model), lambda i: (i, 0))
+    before = [] if held is None else [held]
+    return pl.pallas_call(
+        finish_kernel,
+        out_shape=jax.ShapeDtypeStruct((n_micro * n_seq * seq_len, d_model), jnp.bfloat16),
+        grid=(unit.count * 2,),
+        in_specs=[pl.BlockSpec(memory_space=pl.ANY)] * len(before) + [rows, rows, rows],
+        out_specs=pl.BlockSpec((block, d_model), lambda i: (base + i, 0)),
+        input_output_aliases={0: 0} if before else {},
+        compiler_params=pltpu.CompilerParams(dimension_semantics=("arbitrary",)),
+        cost_estimate=pl.CostEstimate(flops=3 * unit.count * seq_len * d_model, bytes_accessed=10 * unit.count * seq_len * d_model, transcendentals=0),
+        name="finish_rows",
+    )(*before, h, shared, routed)
 
 
 def solution(mesh):
@@ -394,6 +508,8 @@
     n_src = group_size // 2
     ring_groups = [[2 * k + core for k in range(n_src)] for core in range(2)]
     pair_perm = [(k, k ^ 1) for k in range(group_size)]
+    up_perm = [(k, (k + 2) % group_size) for k in range(group_size)]
+    down_perm = [(k, (k - 2) % group_size) for k in range(group_size)]
 
     def device_step(tokens, expert_ids, route_weights, attn_norm, w_query, w_key, w_value, w_out, ffn_norm, w_gate, w_up, w_down, shared_gate, shared_up, shared_down):
         n_micro, n_seq, seq_len, d_model = tokens.shape
@@ -410,44 +526,41 @@
 
         meta = jnp.concatenate([expert_ids.astype(jnp.float32).transpose(0, 2, 1), route_weights.transpose(0, 2, 1), jnp.zeros((n_micro, 16 - 2 * top_count, n_tok), jnp.float32)], axis=1)
         meta = lax.all_gather(meta.reshape(n_micro * 16, n_tok), "ep", axis=0, tiled=True)
-        meta = meta.reshape(n_src, 2, n_micro, 16, n_tok)
-        meta = lax.dynamic_index_in_dim(meta, me % 2, axis=1, keepdims=False)
-        ids = meta[:, :, :top_count].astype(jnp.int32)
-        all_weights = meta[:, :, top_count : 2 * top_count]
-        from_own = ids - half * me
-        from_other = ids - half * (me ^ 1)
-        local_ids = jnp.where((from_own >= 0) & (from_own < half), from_own, jnp.where((from_other >= 0) & (from_other < half), from_other + half, -1))
+        slots, cols, table = route_rows(meta, me.reshape(1).astype(jnp.int32), half, top_count, n_src, n_micro, n_seq, seq_len)
+        table = jnp.concatenate([table.reshape(-1), jnp.broadcast_to(me.astype(jnp.int32), (PIECE,))])
 
         gains = (attn_norm.reshape(1, d_model), ffn_norm.reshape(1, d_model))
         attn_weights = (w_query.transpose(1, 0, 2), w_key.transpose(1, 0, 2), w_value.transpose(1, 0, 2), w_out)
-        units = unit_list(n_micro, n_seq)
-        hs, zs, gathered, plans = [], [], [], []
-        for micro, first, count in units:
+        units = [Unit(0, q, 1, n_src, n_seq) for q in range(n_seq)] + [Unit(m, 0, n_seq, n_src, n_seq) for m in range(1, n_micro)]
+        hs, zs, gathered = [], [], []
+        for unit in units:
             if zs:
                 tokens, _ = lax.optimization_barrier((tokens, zs[-1]))
-            h, z = attention_rows(tokens, micro, first, count, gains, attn_weights)
-            h, z = (v.reshape(count * seq_len, d_model) for v in (h, z))
-            hs.append(h)
-            zs.append(z)
-            gathered.append(lax.all_gather(z, "ep", axis=0, tiled=True, axis_index_groups=ring_groups))
-            by_seq = lambda v: v[:, micro].reshape(n_src, top_count, n_seq, seq_len)[:, :, first : first + count].transpose(0, 2, 1, 3).reshape(n_src * count, top_count, seq_len)
-            plans.append(route_tables(by_seq(local_ids), by_seq(all_weights), n_local))
-        routed, partial = [], None
-        for k, (table, slot_rows, cols) in enumerate(plans):
+            h, z = attention_rows(tokens, unit.micro, unit.first, unit.count, gains, attn_weights)
+            hs.append(h.reshape(-1, d_model))
+            zs.append(z.reshape(-1, d_model))
+            if unit.count == 1 or not BY_HOPS:
+                gathered.append([lax.all_gather(zs[-1], "ep", axis=0, tiled=True, axis_index_groups=ring_groups)])
+            else:
+                left = [lax.ppermute(z[q], "ep", up_perm) for q in range(n_seq)]
+                right = [lax.ppermute(z[q], "ep", down_perm) for q in range(n_seq)]
+                far = [lax.ppermute(left[q], "ep", up_perm) if q % 2 == 0 else lax.ppermute(right[q], "ep", down_perm) for q in range(n_seq)]
+                gathered.append([z, *left, *right, *far])
+        out, partial = None, None
+        routed, shared = [], []
+        for k, unit in enumerate(units):
             if partial is not None:
                 table, _ = lax.optimization_barrier((table, partial))
-            x_rows = gather_rows(table, slot_rows, gathered[k], n_local, top_count, max_rows)
-            seg_rows = min(slot_cap, seq_len) * n_src * units[k][2] if units[k][2] == 1 else (slot_cap + SEG * units[k][2]) * n_src
-            y_rows = expert_rows(table, x_rows, own, other, -(-seg_rows // ROWS) * ROWS)
-            partial = combine_rows(table, cols, y_rows, n_local, top_count)
+            x_rows = gather_rows(unit, table, slots, gathered[k], n_local, top_count, max_rows)
+            seg_rows = (slot_cap + (SEG * unit.count if unit.count > 1 else 0)) * n_src
+            y_rows = expert_rows(unit, table, x_rows, own, other, -(-seg_rows // ROWS) * ROWS)
+            partial = combine_rows(unit, table, cols, y_rows, n_local, top_count)
             routed.append(lax.psum_scatter(partial, "ep", scatter_dimension=0, tiled=True, axis_index_groups=ring_groups))
-        outs = [[] for _ in range(n_micro)]
-        for k, (micro, first, count) in enumerate(units):
-            z = zs[k]
-            shared_out = swiglu(z, shared_gate, shared_up, shared_down)
-            layer_rows = hs[k].astype(jnp.float32) + shared_out.astype(jnp.float32) + routed[k]
-            outs[micro].append(layer_rows.astype(jnp.bfloat16).reshape(count, seq_len, d_model))
-        return jnp.stack([jnp.concatenate(parts, axis=0) if len(parts) > 1 else parts[0] for parts in outs])
+        for k, unit in enumerate(units):
+            shared.append(swiglu(zs[k], shared_gate, shared_up, shared_down))
+        for k, unit in enumerate(units):
+            out = finish_rows(unit, out, hs[k], shared[k], routed[k], tokens.shape)
+        return out.reshape(tokens.shape)
 
     token_spec = P(None, ("dp", "ep"), None, None)
     route_spec = P(None, ("dp", "ep"), None)

time: 792 us -> 922 us (1.16)
  waiting for transfers between devices: 198 us -> 362 us
  other arithmetic: 32.4 us -> 1.72 us
  local copies, waits for them, and re-layouts: 24.4 us -> 9.55 us
    ppermute x0 -> x6, waiting for transfers between devices: none -> 169 us  [the longest x2 66.8 us: device_step(): left = [lax.ppermute(z[q], 'ep', up_perm) for q in range(n_seq)]]
    pallas_call x9 -> x13, Pallas kernels: 350 us -> 386 us  [the longest x3 166 us: expert_rows(): pl.pallas_call(functools.partial(expert_kernel, unit, n_local), out_shape...]
    pallas_call x3, Pallas kernels: 119 us -> 89 us  [attention_rows(): pl.pallas_call(attention_kernel, out_shape=(out, out), grid=(n_heads // p...]
    ppermute x3, waiting for transfers between devices: 29.3 us -> 0.01 us  [device_step(): other = tuple((lax.ppermute(w, 'ep', pair_perm) for w in own))]
    all_gather x3 -> x2, waiting for transfers between devices: 0.01 us -> 27 us  [device_step(): lax.all_gather(zs[-1], 'ep', axis=0, tiled=True, axis_index_groups=ring_g...]
  transfers between devices with their start and end apart: 10 -> 15, of which waited for: 3 -> 7; matrix products, arithmetic and copies ran while one was open for 11% -> 5% of each run, Pallas kernels for 60% -> 51%
where the time goes in v3:
time: 922 us; the launch traced here: 914 us
  Pallas kernels  475 us (52%)
  waiting for transfers between devices  362 us (39%)
  matrix products  43 us (5%)
  between operations  13.9 us (2%)
  local copies, waits for them, and re-layouts  9.55 us (1%)
    reduce_scatter x3, waiting for transfers between devices, device_step(): lax.psum_scatter(partial, 'ep', scatter_dimension=0, tiled=True, axis_ind...  166 us
    pallas_call x3, Pallas kernels, expert_rows(): pl.pallas_call(functools.partial(expert_kernel, unit, n_local), out_shape...  166 us
    pallas_call x3, Pallas kernels, combine_rows(): pl.pallas_call(functools.partial(combine_kernel, unit, n_local, top_count...  134 us
    pallas_call x3, Pallas kernels, attention_rows(): pl.pallas_call(attention_kernel, out_shape=(out, out), grid=(n_heads // p...  89 us
    ppermute x2, waiting for transfers between devices, device_step(): left = [lax.ppermute(z[q], 'ep', up_perm) for q in range(n_seq)]  66.8 us
    ppermute x2, waiting for transfers between devices, device_step(): right = [lax.ppermute(z[q], 'ep', down_perm) for q in range(n_seq)]  65.7 us
    pallas_call x3, Pallas kernels, gather_rows(): pl.pallas_call(functools.partial(gather_kernel, unit, n_local, top_count)...  59.4 us
    ppermute x1, waiting for transfers between devices, device_step(): lax.ppermute(right[q], 'ep', down_perm)  36.7 us
  transfers between devices with their start and end apart: 15, of which 7 were waited for; matrix products, arithmetic and copies ran while one was open for 5% of the time, Pallas kernels for 51%

profile of v3, /device:TPU:112, one launch (start us, length us, event | category | flops | bytes accessed | tf_op | source)
XLA Modules:
  0.0 914.2 jit_solution(1129513407080596664)
XLA Ops:
  11.8 23.3 %attention_rows.3 = (bf16[1,512,1536]{2,1,0:T(8,128)(2,1)}, bf16[1,512,1536]{2,1,0:T(8,128)(2,1)}) custom-call(bf16[1,1536]{1,0:T(2,128)(2,1)} %reshape.36.gain_ref, bf16[1,1536]{1,0:T(2,128)(2,1)} %reshape.37.ffn_gain_ref, bf16[2,2,512,1536]{3,2,1,0:T(8,128)(2,1)} %x_ref.3, bf16[12,1536,128]{2,1,0:T(8,128)(2,1)} %bitcast.53, ...), custom_call_target="tpu_custom_call" | custom-call | flops 9663676416 | bytes 30000000 | tf_op jit(solution)/shard_map/attention_rows/pallas_call | solution.py:88
  36.0 23.3 %attention_rows.4 = (bf16[1,512,1536]{2,1,0:T(8,128)(2,1)}, bf16[1,512,1536]{2,1,0:T(8,128)(2,1)}) custom-call(bf16[1,1536]{1,0:T(2,128)(2,1)} %reshape.36.gain_ref, bf16[1,1536]{1,0:T(2,128)(2,1)} %reshape.37.ffn_gain_ref, bf16[2,2,512,1536]{3,2,1,0:T(8,128)(2,1)} %x_ref.3, bf16[12,1536,128]{2,1,0:T(8,128)(2,1)} %bitcast.54, ...), custom_call_target="tpu_custom_call" | custom-call | flops 9663676416 | bytes 30000000 | tf_op jit(solution)/shard_map/attention_rows/pallas_call | solution.py:88
  59.7 11.5 %route_rows.1 = (s32[2,4,2,8,512]{4,3,2,1,0:T(8,128)}, f32[2,4,2,16,512]{4,3,2,1,0:T(8,128)}, s32[2,4,2,8,128]{4,3,2,1,0:T(8,128)}) custom-call(s32[1]{0:T(128)} %bitcast.5.me_ref, f32[256,1024]{1,0:T(8,128)} %all-gather.6.cloned.1.call-done.meta_ref), custom_call_target="tpu_custom_call" | custom-call | flops 500000000 | bytes 2000000 | tf_op jit(solution)/shard_map/route_rows/pallas_call | solution.py:156
  72.7 27.0 %all-gather.8.cloned.1.call-done = bf16[1,2048,1536]{2,1,0:T(8,128)(2,1)} async-done(((bf16[1,512,1536]{2,1,0:T(8,128)(2,1)}), bf16[1,2048,1536]{2,1,0:T(8,128)(2,1)}) %all-gather.8.cloned.1.call-update) | async-done | bytes 6291472 | tf_op jit(solution)/shard_map/all_gather | solution.py:543
  99.7 15.6 %gather_rows.3.x_hbm = bf16[4,3072,1536]{2,1,0:T(8,128)(2,1)} custom-call(s32[17408]{0:T(1024)} %concatenate.7.table_ref, s32[2,4,2,8,512]{4,3,2,1,0:T(8,128)} %get-tuple-element.22.slots_ref, bf16[2048,1536]{1,0:T(8,128)(2,1)} %bitcast.46), custom_call_target="tpu_custom_call" | custom-call | flops 6442450944 | bytes 18874368 | tf_op jit(solution)/shard_map/gather_rows/pallas_call | solution.py:272
  115.4 49.2 %expert_rows.3.y_hbm = bf16[4,3072,1536]{2,1,0:T(8,128)(2,1)} custom-call(s32[17408]{0:T(1024)} %concatenate.7.table_ref, bf16[4,3072,1536]{2,1,0:T(8,128)(2,1)} %gather_rows.3.x_hbm, bf16[8,1536,512]{2,1,0:T(8,128)(2,1)} %ga.5, bf16[8,1536,512]{2,1,0:T(8,128)(2,1)} %ua.5, bf16[8,512,1536]{2,1,0:T(8,128)(2,1)} %da.5, ...), custom_call_target="tpu_custom_call" | custom-call | flops 38654705664 | bytes 115000000 | tf_op jit(solution)/shard_map/expert_rows/pallas_call | solution.py:355
  164.6 34.5 %combine_rows.3 = f32[2048,1536]{1,0:T(8,128)} custom-call(s32[17408]{0:T(1024)} %concatenate.7.table_ref, f32[2,4,2,16,512]{4,3,2,1,0:T(8,128)} %get-tuple-element.21.cols_ref, bf16[4,3072,1536]{2,1,0:T(8,128)(2,1)} %expert_rows.3.y_hbm), custom_call_target="tpu_custom_call" | custom-call | flops 19327352832 | bytes 25165824 | tf_op jit(solution)/shard_map/combine_rows/pallas_call | solution.py:457
  199.3 15.6 %gather_rows.4.x_hbm = bf16[4,3072,1536]{2,1,0:T(8,128)(2,1)} custom-call(s32[17408]{0:T(1024)} %concatenate.7.table_ref, s32[2,4,2,8,512]{4,3,2,1,0:T(8,128)} %get-tuple-element.22.slots_ref, bf16[2048,1536]{1,0:T(8,128)(2,1)} %bitcast.45), custom_call_target="tpu_custom_call" | custom-call | flops 6442450944 | bytes 18874368 | tf_op jit(solution)/shard_map/gather_rows/pallas_call | solution.py:272
  214.9 49.2 %expert_rows.4.y_hbm = bf16[4,3072,1536]{2,1,0:T(8,128)(2,1)} custom-call(s32[17408]{0:T(1024)} %concatenate.7.table_ref, bf16[4,3072,1536]{2,1,0:T(8,128)(2,1)} %gather_rows.4.x_hbm, bf16[8,1536,512]{2,1,0:T(8,128)(2,1)} %ga.5, bf16[8,1536,512]{2,1,0:T(8,128)(2,1)} %ua.5, bf16[8,512,1536]{2,1,0:T(8,128)(2,1)} %da.5, ...), custom_call_target="tpu_custom_call" | custom-call | flops 38654705664 | bytes 115000000 | tf_op jit(solution)/shard_map/expert_rows/pallas_call | solution.py:355
  264.1 34.5 %combine_rows.4 = f32[2048,1536]{1,0:T(8,128)} custom-call(s32[17408]{0:T(1024)} %concatenate.7.table_ref, f32[2,4,2,16,512]{4,3,2,1,0:T(8,128)} %get-tuple-element.21.cols_ref, bf16[4,3072,1536]{2,1,0:T(8,128)(2,1)} %expert_rows.4.y_hbm), custom_call_target="tpu_custom_call" | custom-call | flops 19327352832 | bytes 25165824 | tf_op jit(solution)/shard_map/combine_rows/pallas_call | solution.py:457
  299.3 42.5 %attention_rows.5 = (bf16[2,512,1536]{2,1,0:T(8,128)(2,1)}, bf16[2,512,1536]{2,1,0:T(8,128)(2,1)}) custom-call(bf16[1,1536]{1,0:T(2,128)(2,1)} %reshape.36.gain_ref, bf16[1,1536]{1,0:T(2,128)(2,1)} %reshape.37.ffn_gain_ref, bf16[2,2,512,1536]{3,2,1,0:T(8,128)(2,1)} %x_ref.3, bf16[12,1536,128]{2,1,0:T(8,128)(2,1)} %bitcast.55, ...), custom_call_target="tpu_custom_call" | custom-call | flops 19327352832 | bytes 30000000 | tf_op jit(solution)/shard_map/attention_rows/pallas_call | solution.py:88
  349.3 65.7 %collective-permute-done.6.refs_4_ = bf16[512,1536]{1,0:T(8,128)(2,1)S(1)} collective-permute-done((bf16[512,1536]{1,0:T(8,128)(2,1)S(1)}, bf16[512,1536]{1,0:T(8,128)(2,1)S(1)}, u32[]{:S(2)}, u32[]{:S(2)}) %collective-permute-start.6) | collective-permute-done | bytes 1572896 | tf_op jit(solution)/shard_map/ppermute | solution.py:546
  417.0 66.7 %collective-permute-done.4.refs_2_ = bf16[512,1536]{1,0:T(8,128)(2,1)S(1)} collective-permute-done((bf16[512,1536]{1,0:T(8,128)(2,1)S(1)}, bf16[512,1536]{1,0:T(8,128)(2,1)S(1)}, u32[]{:S(2)}, u32[]{:S(2)}) %collective-permute-start.4) | collective-permute-done | bytes 1572896 | tf_op jit(solution)/shard_map/ppermute | solution.py:545
  483.7 36.7 %collective-permute-done.8.refs_6_ = bf16[512,1536]{1,0:T(8,128)(2,1)S(1)} collective-permute-done((bf16[512,1536]{1,0:T(8,128)(2,1)S(1)}, bf16[512,1536]{1,0:T(8,128)(2,1)S(1)}, u32[]{:S(2)}, u32[]{:S(2)}) %collective-permute-start.8) | collective-permute-done | bytes 1572896 | tf_op jit(solution)/shard_map/ppermute | solution.py:547
  521.7 28.1 %gather_rows.5.x_hbm = bf16[8,3072,1536]{2,1,0:T(8,128)(2,1)} custom-call(s32[17408]{0:T(1024)} %concatenate.7.table_ref, s32[2,4,2,8,512]{4,3,2,1,0:T(8,128)} %get-tuple-element.22.slots_ref, bf16[2,512,1536]{2,1,0:T(8,128)(2,1)} %get-tuple-element.29.refs_0_, bf16[512,1536]{1,0:T(8,128)(2,1)} %copy-done.4, bf16[512,1536]{1,0:T(8,128)(2,1)} %copy-done.5, ...), custom_call_target="tpu_custom_call" | custom-call | flops 12884901888 | bytes 37748736 | tf_op jit(solution)/shard_map/gather_rows/pallas_call | solution.py:272
  549.9 67.3 %expert_rows.5.y_hbm = bf16[8,3072,1536]{2,1,0:T(8,128)(2,1)} custom-call(s32[17408]{0:T(1024)} %concatenate.7.table_ref, bf16[8,3072,1536]{2,1,0:T(8,128)(2,1)} %gather_rows.5.x_hbm, bf16[8,1536,512]{2,1,0:T(8,128)(2,1)} %ga.5, bf16[8,1536,512]{2,1,0:T(8,128)(2,1)} %ua.5, bf16[8,512,1536]{2,1,0:T(8,128)(2,1)} %da.5, ...), custom_call_target="tpu_custom_call" | custom-call | flops 38654705664 | bytes 115000000 | tf_op jit(solution)/shard_map/expert_rows/pallas_call | solution.py:355
  617.2 65.0 %combine_rows.5 = f32[4096,1536]{1,0:T(8,128)} custom-call(s32[17408]{0:T(1024)} %concatenate.7.table_ref, f32[2,4,2,16,512]{4,3,2,1,0:T(8,128)} %get-tuple-element.21.cols_ref, bf16[8,3072,1536]{2,1,0:T(8,128)(2,1)} %expert_rows.5.y_hbm), custom_call_target="tpu_custom_call" | custom-call | flops 38654705664 | bytes 50331648 | tf_op jit(solution)/shard_map/combine_rows/pallas_call | solution.py:457
  683.6 5.1 fusion.2
  692.0 4.9 fusion.11
  696.9 8.5 convolution_convert_fusion.1.refs_2_
  705.4 8.7 convolution_convert_fusion.2.refs_1_
  714.1 12.5 %convolution_convert_fusion.refs_2_ = bf16[1024,1536]{1,0:T(8,128)(2,1)} fusion(bf16[1024,1536]{1,0:T(8,128)(2,1)} %param.29, f32[1024,1024]{1,0:T(8,128)} %fusion.11, bf16[1024,1536]{1,0:T(8,128)(2,1)S(1)} %bitcast.44, bf16[1536,1024]{1,0:T(8,128)(2,1)} %param.28), kind=kOutput, calls=%fused_computation.1 | convolution fusion | flops 6450315264 | bytes 16777216 | tf_op jit(solution)/shard_map/dot_general | solution.py:105
  734.7 165.8 %reduce-scatter.8.cloned.1.call-done.refs_3_ = f32[1024,1536]{1,0:T(8,128)} async-done(((f32[4096,1536]{1,0:T(8,128)}), f32[1024,1536]{1,0:T(8,128)}) %reduce-scatter.8.cloned.1.call-update) | async-done | bytes 6291472 | tf_op jit(solution)/shard_map/reduce_scatter | solution.py:558
  900.4 6.8 finish_rows.5
  (61 shorter events, 32.3 us)
Async XLA Ops:
  6.5 53.1 %all-gather.6.cloned.1.call-start = ((), (), s32[]{:S(2)}) async-start(), calls=%async_computation.3 | async-start | bytes 1179648 | tf_op jit(solution)/shard_map/all_gather | solution.py:528
  9.1 90.6 %all-gather.8.cloned.1.call-start = ((), (), s32[]{:S(2)}) async-start(), calls=%async_computation.7 | async-start | bytes 7864320 | tf_op jit(solution)/shard_map/all_gather | solution.py:543
  35.1 164.2 %all-gather.10.cloned.1.call-start = ((), (), s32[]{:S(2)}) async-start(), calls=%async_computation.8 | async-start | bytes 7864320 | tf_op jit(solution)/shard_map/all_gather | solution.py:543
  35.3 80.0 %collective-permute-start = (bf16[8,1536,512]{2,1,0:T(8,128)(2,1)}, bf16[8,1536,512]{2,1,0:T(8,128)(2,1)}, u32[]{:S(2)}, u32[]{:S(2)}) collective-permute-start(bf16[8,1536,512]{2,1,0:T(8,128)(2,1)} %ga.5), channel_id=1, source_target_pairs={{0,1},{1,0},{2,3},{3,2},{4,5},{5,4},{6,7},{7,6},{8,9},{9,8},{10,11... | collective-permute-start | bytes 37748744 | tf_op jit(solution)/shard_map/ppermute | solution.py:525
  35.4 79.9 %collective-permute-start.1 = (bf16[8,1536,512]{2,1,0:T(8,128)(2,1)}, bf16[8,1536,512]{2,1,0:T(8,128)(2,1)}, u32[]{:S(2)}, u32[]{:S(2)}) collective-permute-start(bf16[8,1536,512]{2,1,0:T(8,128)(2,1)} %ua.5), channel_id=1, source_target_pairs={{0,1},{1,0},{2,3},{3,2},{4,5},{5,4},{6,7},{7,6},{8,9},{9,8},{10,11... | collective-permute-start | bytes 37748744 | tf_op jit(solution)/shard_map/ppermute | solution.py:525
  35.9 79.5 %collective-permute-start.2 = (bf16[8,512,1536]{2,1,0:T(8,128)(2,1)}, bf16[8,512,1536]{2,1,0:T(8,128)(2,1)}, u32[]{:S(2)}, u32[]{:S(2)}) collective-permute-start(bf16[8,512,1536]{2,1,0:T(8,128)(2,1)} %da.5), channel_id=1, source_target_pairs={{0,1},{1,0},{2,3},{3,2},{4,5},{5,4},{6,7},{7,6},{8,9},{9,8},{10,11... | collective-permute-start | bytes 37748744 | tf_op jit(solution)/shard_map/ppermute | solution.py:525
  59.3 667.3 %reduce-scatter.4.cloned.1.call-start = ((), (), s32[]{:S(2)}) async-start(), calls=%async_computation.4 | async-start | bytes 15728640 | tf_op jit(solution)/shard_map/reduce_scatter | solution.py:558
  199.2 531.5 %reduce-scatter.6.cloned.1.call-start = ((), (), s32[]{:S(2)}) async-start(), calls=%async_computation.5 | async-start | bytes 15728640 | tf_op jit(solution)/shard_map/reduce_scatter | solution.py:558
  298.7 601.7 %reduce-scatter.8.cloned.1.call-start = ((), (), s32[]{:S(2)}) async-start(), calls=%async_computation.6 | async-start | bytes 31457280 | tf_op jit(solution)/shard_map/reduce_scatter | solution.py:558
  343.9 71.0 %collective-permute-start.6 = (bf16[512,1536]{1,0:T(8,128)(2,1)S(1)}, bf16[512,1536]{1,0:T(8,128)(2,1)S(1)}, u32[]{:S(2)}, u32[]{:S(2)}) collective-permute-start(bf16[512,1536]{1,0:T(8,128)(2,1)S(1)} %get-tuple-element.31), channel_id=1, source_target_pairs={{0,6},{1,7},{2,0},{3,1},{4,2},{5,3},{6,4},{7,5},{8,14},{9,15},{10,... | collective-permute-start | bytes 4718600 | tf_op jit(solution)/shard_map/ppermute | solution.py:546
  344.0 72.3 %collective-permute-start.3 = (bf16[512,1536]{1,0:T(8,128)(2,1)S(1)}, bf16[512,1536]{1,0:T(8,128)(2,1)S(1)}, u32[]{:S(2)}, u32[]{:S(2)}) collective-permute-start(bf16[512,1536]{1,0:T(8,128)(2,1)S(1)} %get-tuple-element.32), channel_id=1, source_target_pairs={{0,2},{1,3},{2,4},{3,5},{4,6},{5,7},{6,0},{7,1},{8,10},{9,11},{10,... | collective-permute-start | bytes 4718600 | tf_op jit(solution)/shard_map/ppermute | solution.py:545
  346.0 137.7 %collective-permute-start.4 = (bf16[512,1536]{1,0:T(8,128)(2,1)S(1)}, bf16[512,1536]{1,0:T(8,128)(2,1)S(1)}, u32[]{:S(2)}, u32[]{:S(2)}) collective-permute-start(bf16[512,1536]{1,0:T(8,128)(2,1)S(1)} %get-tuple-element.31), channel_id=1, source_target_pairs={{0,2},{1,3},{2,4},{3,5},{4,6},{5,7},{6,0},{7,1},{8,10},{9,11},{10,... | collective-permute-start | bytes 4718600 | tf_op jit(solution)/shard_map/ppermute | solution.py:545
  347.4 136.3 %collective-permute-start.5 = (bf16[512,1536]{1,0:T(8,128)(2,1)S(1)}, bf16[512,1536]{1,0:T(8,128)(2,1)S(1)}, u32[]{:S(2)}, u32[]{:S(2)}) collective-permute-start(bf16[512,1536]{1,0:T(8,128)(2,1)S(1)} %get-tuple-element.32), channel_id=1, source_target_pairs={{0,6},{1,7},{2,0},{3,1},{4,2},{5,3},{6,4},{7,5},{8,14},{9,15},{10,... | collective-permute-start | bytes 4718600 | tf_op jit(solution)/shard_map/ppermute | solution.py:546
  415.0 106.8 %copy-start.3 = (bf16[512,1536]{1,0:T(8,128)(2,1)}, bf16[512,1536]{1,0:T(8,128)(2,1)S(1)}, u32[]{:S(2)}) copy-start(bf16[512,1536]{1,0:T(8,128)(2,1)S(1)} %collective-permute-done.6.refs_4_) | copy-start | bytes 4718596
  415.0 105.4 %collective-permute-start.8 = (bf16[512,1536]{1,0:T(8,128)(2,1)S(1)}, bf16[512,1536]{1,0:T(8,128)(2,1)S(1)}, u32[]{:S(2)}, u32[]{:S(2)}) collective-permute-start(bf16[512,1536]{1,0:T(8,128)(2,1)S(1)} %collective-permute-done.6.refs_4_), channel_id=1, source_target_pairs={{0,6},{1,7},{2,0},{3,1},{4,2},{5,3},{6,4},{7,5},{8,14},{9,15},{10,... | collective-permute-start | bytes 4718600 | tf_op jit(solution)/shard_map/ppermute | solution.py:547
  416.3 104.1 %copy-start.4 = (bf16[512,1536]{1,0:T(8,128)(2,1)}, bf16[512,1536]{1,0:T(8,128)(2,1)S(1)}, u32[]{:S(2)}) copy-start(bf16[512,1536]{1,0:T(8,128)(2,1)S(1)} %collective-permute-done.3.refs_1_) | copy-start | bytes 4718596
  416.3 105.4 %collective-permute-start.7 = (bf16[512,1536]{1,0:T(8,128)(2,1)S(1)}, bf16[512,1536]{1,0:T(8,128)(2,1)}, u32[]{:S(2)}, u32[]{:S(2)}) collective-permute-start(bf16[512,1536]{1,0:T(8,128)(2,1)S(1)} %collective-permute-done.3.refs_1_), channel_id=1, source_target_pairs={{0,2},{1,3},{2,4},{3,5},{4,6},{5,7},{6,0},{7,1},{8,10},{9,11},{10,... | collective-permute-start | bytes 4718600 | tf_op jit(solution)/shard_map/ppermute | solution.py:547
  483.7 36.7 %copy-start.5 = (bf16[512,1536]{1,0:T(8,128)(2,1)}, bf16[512,1536]{1,0:T(8,128)(2,1)S(1)}, u32[]{:S(2)}) copy-start(bf16[512,1536]{1,0:T(8,128)(2,1)S(1)} %collective-permute-done.4.refs_2_) | copy-start | bytes 4718596
  483.7 36.7 %copy-start.6 = (bf16[512,1536]{1,0:T(8,128)(2,1)}, bf16[512,1536]{1,0:T(8,128)(2,1)S(1)}, u32[]{:S(2)}) copy-start(bf16[512,1536]{1,0:T(8,128)(2,1)S(1)} %collective-permute-done.5.refs_3_) | copy-start | bytes 4718596
  520.4 1.2 copy-start.7
  682.2 1.4 copy-start.2
  683.6 5.1 copy-start.1
  683.6 5.1 copy-start.8
  688.7 3.2 copy-start
Sparse Core Ops, SparseCore 0:
  9.2 22.0 all-gather.5
  35.2 64.4 all-gather.7
  101.3 62.1 all-gather.9
  199.3 110.4 reduce-scatter.3
  312.0 182.8 reduce-scatter.5
  682.4 217.9 reduce-scatter.7

commit v4 on v3

--- a/solution.py
+++ b/solution.py
@@ -30,15 +30,16 @@
     return (wide_vals * inv_rms * norm_gain.astype(jnp.float32)).astype(jnp.bfloat16)
 
 
-def attention_kernel(gain_ref, ffn_gain_ref, x_ref, wq_ref, wk_ref, wv_ref, wo_ref, h_ref, z_ref, normed, acc):
+def attention_kernel(gains_ref, x_ref, wq_ref, wk_ref, wv_ref, wo_ref, h_ref, *refs):
     group, seq = pl.program_id(0), pl.program_id(1)
+    *z_refs, normed, acc = refs
     seq_len, d_model = normed.shape[1:]
     per, _, head_dim = wq_ref.shape
     block = seq_len // Q_BLOCKS
 
     @pl.when(group == 0)
     def _():
-        normed[seq] = rms_norm(x_ref[0, seq], gain_ref[...])
+        normed[seq] = rms_norm(x_ref[0, seq], gains_ref[0:1, :])
 
     rows = normed[seq]
     project = lambda w_ref: jnp.dot(rows, jnp.concatenate([w_ref[i] for i in range(per)], axis=1), preferred_element_type=jnp.float32).astype(jnp.bfloat16)
@@ -73,7 +74,12 @@
     def _():
         residual = (x_ref[0, seq].astype(jnp.float32) + acc[seq]).astype(jnp.bfloat16)
         h_ref[seq] = residual
-        z_ref[seq] = rms_norm(residual, ffn_gain_ref[...])
+        z = rms_norm(residual, gains_ref[1:2, :])
+        for i, z_ref in enumerate(z_refs):
+
+            @pl.when(seq == i)
+            def _():
+                z_ref[...] = z
 
 
 def attention_rows(tokens, micro, first, n_seq, gains, weights):
@@ -82,20 +88,21 @@
     per = 4 if n_heads % 4 == 0 else 1
     out = jax.ShapeDtypeStruct((n_seq, seq_len, d_model), jnp.bfloat16)
     whole = pl.BlockSpec((n_seq, seq_len, d_model), lambda g, s: (0, 0, 0))
-    gain = pl.BlockSpec((1, d_model), lambda g, s: (0, 0))
+    gain = pl.BlockSpec((2, d_model), lambda g, s: (0, 0))
+    z_out = pl.BlockSpec((seq_len, d_model), lambda g, s: (0, 0))
     in_w = pl.BlockSpec((per, d_model, head_dim), lambda g, s: (g, 0, 0))
     rows = n_seq * seq_len
     return pl.pallas_call(
         attention_kernel,
-        out_shape=(out, out),
+        out_shape=(out, *[jax.ShapeDtypeStruct((seq_len, d_model), jnp.bfloat16)] * n_seq),
         grid=(n_heads // per, n_seq),
-        in_specs=[gain, gain, pl.BlockSpec((1, n_seq, seq_len, d_model), lambda g, s: (micro, first // n_seq, 0, 0)), in_w, in_w, in_w, pl.BlockSpec((per, head_dim, d_model), lambda g, s: (g, 0, 0))],
-        out_specs=(whole, whole),
+        in_specs=[gain, pl.BlockSpec((1, n_seq, seq_len, d_model), lambda g, s: (micro, first // n_seq, 0, 0)), in_w, in_w, in_w, pl.BlockSpec((per, head_dim, d_model), lambda g, s: (g, 0, 0))],
+        out_specs=(whole, *[z_out] * n_seq),
         scratch_shapes=[pltpu.VMEM((n_seq, seq_len, d_model), jnp.bfloat16), pltpu.VMEM((n_seq, seq_len, d_model), jnp.float32)],
         compiler_params=pltpu.CompilerParams(dimension_semantics=("arbitrary", "arbitrary"), vmem_limit_bytes=VMEM_LIMIT),
         cost_estimate=pl.CostEstimate(flops=8 * rows * d_model * d_model, bytes_accessed=30_000_000, transcendentals=0),
         name="attention_rows",
-    )(*gains, tokens, *weights)
+    )(gains, tokens, *weights)
 
 
 def swiglu(in_rows, gate_w, up_w, down_w):
@@ -203,9 +210,9 @@
         def fetch(i):
             _, s, q = unit.spot(i)
             away = lax.rem(s - x_at + unit.n_src, unit.n_src)
-            own, left, right, far = z_refs[0], z_refs[1:3], z_refs[3:5], z_refs[5:7]
+            own, left, right, far = (z_refs[g * unit.count : (g + 1) * unit.count] for g in range(4))
             for seq in range(unit.count):
-                for hop, ref in enumerate((own.at[seq], right[seq], far[seq], left[seq])):
+                for hop, ref in enumerate((own[seq], right[seq], far[seq], left[seq])):
 
                     @pl.when((q == seq) & (away == hop))
                     def _():
@@ -316,19 +323,26 @@
 
     slot = lax.rem(step, 2)
     total = unit.field(table_ref, unit.pieces - 1, 1, step) + unit.field(table_ref, unit.pieces - 1, 2, step)
-    n_blocks = (total + ROWS - 1) // ROWS
+    n_blocks = (total + ROWS // 2 - 1) // ROWS
 
     def run(gate, up, down):
-        def block(c, carry):
-            rows = pl.ds(pl.multiple_of(c * ROWS, ROWS), ROWS)
+        def feed(start, size):
+            rows = pl.ds(pl.multiple_of(start, ROWS), size)
             x = x_buf[slot, rows, :]
             g = jnp.dot(x, gate[0], preferred_element_type=jnp.float32)
             u = jnp.dot(x, up[0], preferred_element_type=jnp.float32)
             h = (g * jax.nn.sigmoid(g) * u).astype(jnp.bfloat16)
             y_buf[slot, rows, :] = jnp.dot(h, down[0], preferred_element_type=jnp.float32).astype(jnp.bfloat16)
+
+        def block(c, carry):
+            feed(c * ROWS, ROWS)
             return carry
 
         lax.fori_loop(0, n_blocks, block, 0)
+
+        @pl.when(total > n_blocks * ROWS)
+        def _():
+            feed(n_blocks * ROWS, ROWS // 2)
 
     @pl.when(step < n_local // 2)
     def _():
@@ -529,23 +543,23 @@
         slots, cols, table = route_rows(meta, me.reshape(1).astype(jnp.int32), half, top_count, n_src, n_micro, n_seq, seq_len)
         table = jnp.concatenate([table.reshape(-1), jnp.broadcast_to(me.astype(jnp.int32), (PIECE,))])
 
-        gains = (attn_norm.reshape(1, d_model), ffn_norm.reshape(1, d_model))
+        gains = jnp.stack([attn_norm, ffn_norm]).astype(jnp.float32)
         attn_weights = (w_query.transpose(1, 0, 2), w_key.transpose(1, 0, 2), w_value.transpose(1, 0, 2), w_out)
         units = [Unit(0, q, 1, n_src, n_seq) for q in range(n_seq)] + [Unit(m, 0, n_seq, n_src, n_seq) for m in range(1, n_micro)]
         hs, zs, gathered = [], [], []
         for unit in units:
             if zs:
-                tokens, _ = lax.optimization_barrier((tokens, zs[-1]))
-            h, z = attention_rows(tokens, unit.micro, unit.first, unit.count, gains, attn_weights)
+                tokens, _ = lax.optimization_barrier((tokens, zs[-1][0]))
+            h, *z = attention_rows(tokens, unit.micro, unit.first, unit.count, gains, attn_weights)
             hs.append(h.reshape(-1, d_model))
-            zs.append(z.reshape(-1, d_model))
+            zs.append(z)
             if unit.count == 1 or not BY_HOPS:
-                gathered.append([lax.all_gather(zs[-1], "ep", axis=0, tiled=True, axis_index_groups=ring_groups)])
+                gathered.append([lax.all_gather(jnp.concatenate(z) if unit.count > 1 else z[0], "ep", axis=0, tiled=True, axis_index_groups=ring_groups)])
             else:
                 left = [lax.ppermute(z[q], "ep", up_perm) for q in range(n_seq)]
                 right = [lax.ppermute(z[q], "ep", down_perm) for q in range(n_seq)]
                 far = [lax.ppermute(left[q], "ep", up_perm) if q % 2 == 0 else lax.ppermute(right[q], "ep", down_perm) for q in range(n_seq)]
-                gathered.append([z, *left, *right, *far])
+                gathered.append([*z, *left, *right, *far])
         out, partial = None, None
         routed, shared = [], []
         for k, unit in enumerate(units):
@@ -557,7 +571,7 @@
             partial = combine_rows(unit, table, cols, y_rows, n_local, top_count)
             routed.append(lax.psum_scatter(partial, "ep", scatter_dimension=0, tiled=True, axis_index_groups=ring_groups))
         for k, unit in enumerate(units):
-            shared.append(swiglu(zs[k], shared_gate, shared_up, shared_down))
+            shared.append(swiglu(jnp.concatenate(zs[k]) if unit.count > 1 else zs[k][0], shared_gate, shared_up, shared_down))
         for k, unit in enumerate(units):
             out = finish_rows(unit, out, hs[k], shared[k], routed[k], tokens.shape)
         return out.reshape(tokens.shape)

time: 922 us -> 914 us (level)
  Pallas kernels: 475 us -> 463 us
    ppermute x1, waiting for transfers between devices: 0.14 us -> 40.8 us  [device_step(): lax.ppermute(left[q], 'ep', up_perm)]
    ppermute x1, waiting for transfers between devices: 36.7 us -> 0.01 us  [device_step(): lax.ppermute(right[q], 'ep', down_perm)]
    pallas_call x3, Pallas kernels: 166 us -> 154 us  [expert_rows(): pl.pallas_call(functools.partial(expert_kernel, unit, n_local), out_shape...]
  transfers between devices with their start and end apart: 15 -> 15, of which waited for: 7 -> 5; matrix products, arithmetic and copies ran while one was open for 5% -> 5% of each run, Pallas kernels for 51% -> 50%
where the time goes in v4:
time: 914 us; the launch traced here: 905 us
  Pallas kernels  463 us (51%)
  waiting for transfers between devices  366 us (40%)
  matrix products  39.6 us (4%)
  between operations  13.9 us (2%)
  starting transfers between devices  11.5 us (1%)
    reduce_scatter x3, waiting for transfers between devices, device_step(): lax.psum_scatter(partial, 'ep', scatter_dimension=0, tiled=True, axis_ind...  165 us
    pallas_call x3, Pallas kernels, expert_rows(): pl.pallas_call(functools.partial(expert_kernel, unit, n_local), out_shape...  154 us
    pallas_call x3, Pallas kernels, combine_rows(): pl.pallas_call(functools.partial(combine_kernel, unit, n_local, top_count...  134 us
    pallas_call x3, Pallas kernels, attention_rows(): pl.pallas_call(attention_kernel, out_shape=(out, *[jax.ShapeDtypeStruct((...  89.1 us
    ppermute x2, waiting for transfers between devices, device_step(): left = [lax.ppermute(z[q], 'ep', up_perm) for q in range(n_seq)]  66.7 us
    ppermute x2, waiting for transfers between devices, device_step(): right = [lax.ppermute(z[q], 'ep', down_perm) for q in range(n_seq)]  66.2 us
    pallas_call x3, Pallas kernels, gather_rows(): pl.pallas_call(functools.partial(gather_kernel, unit, n_local, top_count)...  59.4 us
    ppermute x1, waiting for transfers between devices, device_step(): lax.ppermute(left[q], 'ep', up_perm)  40.8 us
  transfers between devices with their start and end apart: 15, of which 5 were waited for; matrix products, arithmetic and copies ran while one was open for 5% of the time, Pallas kernels for 50%

profile of v4, /device:TPU:112, one launch (start us, length us, event | category | flops | bytes accessed | tf_op | source)
XLA Modules:
  0.0 905.4 jit_solution(9297020757190232066)
XLA Ops:
  11.2 23.2 %attention_rows.3 = (bf16[1,512,1536]{2,1,0:T(8,128)(2,1)}, bf16[512,1536]{1,0:T(8,128)(2,1)}) custom-call(f32[2,1536]{1,0:T(2,128)} %maximum_convert_fusion.gains_ref, bf16[2,2,512,1536]{3,2,1,0:T(8,128)(2,1)} %x_ref.3, bf16[12,1536,128]{2,1,0:T(8,128)(2,1)} %bitcast.34, bf16[12,1536,128]{2,1,0:T(8,128)(2,1)} %bitcast.37, bf16[12,1536,128]{2,1,0:T(8,128)(2,1)} %bitcast.40, ...), custom_call_target="tpu_custom_call" | custom-call | flops 9663676416 | bytes 30000000 | tf_op jit(solution)/shard_map/attention_rows/pallas_call | solution.py:95
  35.4 23.2 %attention_rows.4 = (bf16[1,512,1536]{2,1,0:T(8,128)(2,1)}, bf16[512,1536]{1,0:T(8,128)(2,1)}) custom-call(f32[2,1536]{1,0:T(2,128)} %maximum_convert_fusion.gains_ref, bf16[2,2,512,1536]{3,2,1,0:T(8,128)(2,1)} %x_ref.3, bf16[12,1536,128]{2,1,0:T(8,128)(2,1)} %bitcast.35, bf16[12,1536,128]{2,1,0:T(8,128)(2,1)} %bitcast.38, bf16[12,1536,128]{2,1,0:T(8,128)(2,1)} %bitcast.41, ...), custom_call_target="tpu_custom_call" | custom-call | flops 9663676416 | bytes 30000000 | tf_op jit(solution)/shard_map/attention_rows/pallas_call | solution.py:95
  59.0 11.5 %route_rows.1 = (s32[2,4,2,8,512]{4,3,2,1,0:T(8,128)}, f32[2,4,2,16,512]{4,3,2,1,0:T(8,128)}, s32[2,4,2,8,128]{4,3,2,1,0:T(8,128)}) custom-call(s32[1]{0:T(128)} %bitcast.4.me_ref, f32[256,1024]{1,0:T(8,128)} %all-gather.4.cloned.1.call-done.meta_ref), custom_call_target="tpu_custom_call" | custom-call | flops 500000000 | bytes 2000000 | tf_op jit(solution)/shard_map/route_rows/pallas_call | solution.py:163
  72.0 27.1 %all-gather.6.cloned.1.call-done.refs_0_ = bf16[2048,1536]{1,0:T(8,128)(2,1)} async-done(((bf16[512,1536]{1,0:T(8,128)(2,1)}), bf16[2048,1536]{1,0:T(8,128)(2,1)}) %all-gather.6.cloned.1.call-update) | async-done | bytes 6291472 | tf_op jit(solution)/shard_map/all_gather | solution.py:557
  99.1 15.6 %gather_rows.3.x_hbm = bf16[4,3072,1536]{2,1,0:T(8,128)(2,1)} custom-call(s32[17408]{0:T(1024)} %concatenate.10.table_ref, s32[2,4,2,8,512]{4,3,2,1,0:T(8,128)} %get-tuple-element.23.slots_ref, bf16[2048,1536]{1,0:T(8,128)(2,1)} %all-gather.6.cloned.1.call-done.refs_0_), custom_call_target="tpu_custom_call" | custom-call | flops 6442450944 | bytes 18874368 | tf_op jit(solution)/shard_map/gather_rows/pallas_call | solution.py:279
  114.8 45.7 %expert_rows.3.y_hbm = bf16[4,3072,1536]{2,1,0:T(8,128)(2,1)} custom-call(s32[17408]{0:T(1024)} %concatenate.10.table_ref, bf16[4,3072,1536]{2,1,0:T(8,128)(2,1)} %gather_rows.3.x_hbm, bf16[8,1536,512]{2,1,0:T(8,128)(2,1)} %ga.5, bf16[8,1536,512]{2,1,0:T(8,128)(2,1)} %ua.5, bf16[8,512,1536]{2,1,0:T(8,128)(2,1)} %da.5, ...), custom_call_target="tpu_custom_call" | custom-call | flops 38654705664 | bytes 115000000 | tf_op jit(solution)/shard_map/expert_rows/pallas_call | solution.py:369
  160.5 34.5 %combine_rows.3 = f32[2048,1536]{1,0:T(8,128)} custom-call(s32[17408]{0:T(1024)} %concatenate.10.table_ref, f32[2,4,2,16,512]{4,3,2,1,0:T(8,128)} %get-tuple-element.22.cols_ref, bf16[4,3072,1536]{2,1,0:T(8,128)(2,1)} %expert_rows.3.y_hbm), custom_call_target="tpu_custom_call" | custom-call | flops 19327352832 | bytes 25165824 | tf_op jit(solution)/shard_map/combine_rows/pallas_call | solution.py:471
  195.4 15.6 %gather_rows.4.x_hbm = bf16[4,3072,1536]{2,1,0:T(8,128)(2,1)} custom-call(s32[17408]{0:T(1024)} %concatenate.10.table_ref, s32[2,4,2,8,512]{4,3,2,1,0:T(8,128)} %get-tuple-element.23.slots_ref, bf16[2048,1536]{1,0:T(8,128)(2,1)} %all-gather.8.cloned.1.call-done.refs_0_), custom_call_target="tpu_custom_call" | custom-call | flops 6442450944 | bytes 18874368 | tf_op jit(solution)/shard_map/gather_rows/pallas_call | solution.py:279
  211.1 45.9 %expert_rows.4.y_hbm = bf16[4,3072,1536]{2,1,0:T(8,128)(2,1)} custom-call(s32[17408]{0:T(1024)} %concatenate.10.table_ref, bf16[4,3072,1536]{2,1,0:T(8,128)(2,1)} %gather_rows.4.x_hbm, bf16[8,1536,512]{2,1,0:T(8,128)(2,1)} %ga.5, bf16[8,1536,512]{2,1,0:T(8,128)(2,1)} %ua.5, bf16[8,512,1536]{2,1,0:T(8,128)(2,1)} %da.5, ...), custom_call_target="tpu_custom_call" | custom-call | flops 38654705664 | bytes 115000000 | tf_op jit(solution)/shard_map/expert_rows/pallas_call | solution.py:369
  257.1 34.6 %combine_rows.4 = f32[2048,1536]{1,0:T(8,128)} custom-call(s32[17408]{0:T(1024)} %concatenate.10.table_ref, f32[2,4,2,16,512]{4,3,2,1,0:T(8,128)} %get-tuple-element.22.cols_ref, bf16[4,3072,1536]{2,1,0:T(8,128)(2,1)} %expert_rows.4.y_hbm), custom_call_target="tpu_custom_call" | custom-call | flops 19327352832 | bytes 25165824 | tf_op jit(solution)/shard_map/combine_rows/pallas_call | solution.py:471
  292.2 42.7 %attention_rows.5 = (bf16[2,512,1536]{2,1,0:T(8,128)(2,1)}, bf16[512,1536]{1,0:T(8,128)(2,1)}, bf16[512,1536]{1,0:T(8,128)(2,1)}) custom-call(f32[2,1536]{1,0:T(2,128)} %maximum_convert_fusion.gains_ref, bf16[2,2,512,1536]{3,2,1,0:T(8,128)(2,1)} %x_ref.3, bf16[12,1536,128]{2,1,0:T(8,128)(2,1)} %bitcast.36, bf16[12,1536,128]{2,1,0:T(8,128)(2,1)} %bitcast.39, ...), custom_call_target="tpu_custom_call" | custom-call | flops 19327352832 | bytes 30000000 | tf_op jit(solution)/shard_map/attention_rows/pallas_call | solution.py:95
  340.7 66.7 %collective-permute-done.3.refs_2_ = bf16[512,1536]{1,0:T(8,128)(2,1)S(1)} collective-permute-done((bf16[512,1536]{1,0:T(8,128)(2,1)}, bf16[512,1536]{1,0:T(8,128)(2,1)S(1)}, u32[]{:S(2)}, u32[]{:S(2)}) %collective-permute-start.3) | collective-permute-done | bytes 1572896 | tf_op jit(solution)/shard_map/ppermute | solution.py:559
  411.0 66.2 %collective-permute-done.5.refs_4_ = bf16[512,1536]{1,0:T(8,128)(2,1)S(1)} collective-permute-done((bf16[512,1536]{1,0:T(8,128)(2,1)}, bf16[512,1536]{1,0:T(8,128)(2,1)S(1)}, u32[]{:S(2)}, u32[]{:S(2)}) %collective-permute-start.5) | collective-permute-done | bytes 1572896 | tf_op jit(solution)/shard_map/ppermute | solution.py:560
  477.3 40.8 %collective-permute-done.7.refs_6_ = bf16[512,1536]{1,0:T(8,128)(2,1)S(1)} collective-permute-done((bf16[512,1536]{1,0:T(8,128)(2,1)S(1)}, bf16[512,1536]{1,0:T(8,128)(2,1)S(1)}, u32[]{:S(2)}, u32[]{:S(2)}) %collective-permute-start.7) | collective-permute-done | bytes 1572896 | tf_op jit(solution)/shard_map/ppermute | solution.py:561
  519.2 28.1 %gather_rows.5.x_hbm = bf16[8,3072,1536]{2,1,0:T(8,128)(2,1)} custom-call(s32[17408]{0:T(1024)} %concatenate.10.table_ref, s32[2,4,2,8,512]{4,3,2,1,0:T(8,128)} %get-tuple-element.23.slots_ref, bf16[512,1536]{1,0:T(8,128)(2,1)} %get-tuple-element.30.refs_0_, bf16[512,1536]{1,0:T(8,128)(2,1)} %get-tuple-element.31.refs_1_, bf16[512,1536]{1,0:T(8,128)(2,1)} %copy-done.4, ...), custom_call_target="tpu_custom_call" | custom-call | flops 12884901888 | bytes 37748736 | tf_op jit(solution)/shard_map/gather_rows/pallas_call | solution.py:279
  547.4 62.3 %expert_rows.5.y_hbm = bf16[8,3072,1536]{2,1,0:T(8,128)(2,1)} custom-call(s32[17408]{0:T(1024)} %concatenate.10.table_ref, bf16[8,3072,1536]{2,1,0:T(8,128)(2,1)} %gather_rows.5.x_hbm, bf16[8,1536,512]{2,1,0:T(8,128)(2,1)} %ga.5, bf16[8,1536,512]{2,1,0:T(8,128)(2,1)} %ua.5, bf16[8,512,1536]{2,1,0:T(8,128)(2,1)} %da.5, ...), custom_call_target="tpu_custom_call" | custom-call | flops 38654705664 | bytes 115000000 | tf_op jit(solution)/shard_map/expert_rows/pallas_call | solution.py:369
  609.7 64.9 %combine_rows.5 = f32[4096,1536]{1,0:T(8,128)} custom-call(s32[17408]{0:T(1024)} %concatenate.10.table_ref, f32[2,4,2,16,512]{4,3,2,1,0:T(8,128)} %get-tuple-element.22.cols_ref, bf16[8,3072,1536]{2,1,0:T(8,128)(2,1)} %expert_rows.5.y_hbm), custom_call_target="tpu_custom_call" | custom-call | flops 38654705664 | bytes 50331648 | tf_op jit(solution)/shard_map/combine_rows/pallas_call | solution.py:471
  685.2 4.9 fusion.5
  690.1 8.1 convolution_convert_fusion.2.refs_1_
  698.2 8.1 convolution_convert_fusion.1.refs_2_
  706.2 12.2 %convolution_convert_fusion.refs_2_ = bf16[1024,1536]{1,0:T(8,128)(2,1)} fusion(bf16[1024,1536]{1,0:T(8,128)(2,1)} %param.29, f32[1024,1024]{1,0:T(8,128)} %fusion.5, bf16[1024,1536]{1,0:T(8,128)(2,1)} %copy-done.9, bf16[1536,1024]{1,0:T(8,128)(2,1)} %param.28), kind=kOutput, calls=%fused_computation.1 | convolution fusion | flops 6450315264 | bytes 16777216 | tf_op jit(solution)/shard_map/dot_general | solution.py:112
  718.5 4.0 finish_rows.3.refs_0_
  726.5 165.1 %reduce-scatter.8.cloned.1.call-done.refs_3_ = f32[1024,1536]{1,0:T(8,128)} async-done(((f32[4096,1536]{1,0:T(8,128)}), f32[1024,1536]{1,0:T(8,128)}) %reduce-scatter.8.cloned.1.call-update) | async-done | bytes 6291472 | tf_op jit(solution)/shard_map/reduce_scatter | solution.py:572
  891.6 6.8 finish_rows.5
  (67 shorter events, 33.5 us)
Async XLA Ops:
  6.5 52.4 %all-gather.4.cloned.1.call-start = ((), (), s32[]{:S(2)}) async-start(), calls=%async_computation.3 | async-start | bytes 1179648 | tf_op jit(solution)/shard_map/all_gather | solution.py:542
  9.1 90.0 %all-gather.6.cloned.1.call-start = ((), (), s32[]{:S(2)}) async-start(), calls=%async_computation.4 | async-start | bytes 7864320 | tf_op jit(solution)/shard_map/all_gather | solution.py:557
  34.5 161.0 %all-gather.8.cloned.1.call-start = ((), (), s32[]{:S(2)}) async-start(), calls=%async_computation.6 | async-start | bytes 7864320 | tf_op jit(solution)/shard_map/all_gather | solution.py:557
  34.7 80.0 %collective-permute-start = (bf16[8,1536,512]{2,1,0:T(8,128)(2,1)}, bf16[8,1536,512]{2,1,0:T(8,128)(2,1)}, u32[]{:S(2)}, u32[]{:S(2)}) collective-permute-start(bf16[8,1536,512]{2,1,0:T(8,128)(2,1)} %ga.5), channel_id=1, source_target_pairs={{0,1},{1,0},{2,3},{3,2},{4,5},{5,4},{6,7},{7,6},{8,9},{9,8},{10,11... | collective-permute-start | bytes 37748744 | tf_op jit(solution)/shard_map/ppermute | solution.py:539
  34.8 79.9 %collective-permute-start.1 = (bf16[8,1536,512]{2,1,0:T(8,128)(2,1)}, bf16[8,1536,512]{2,1,0:T(8,128)(2,1)}, u32[]{:S(2)}, u32[]{:S(2)}) collective-permute-start(bf16[8,1536,512]{2,1,0:T(8,128)(2,1)} %ua.5), channel_id=1, source_target_pairs={{0,1},{1,0},{2,3},{3,2},{4,5},{5,4},{6,7},{7,6},{8,9},{9,8},{10,11... | collective-permute-start | bytes 37748744 | tf_op jit(solution)/shard_map/ppermute | solution.py:539
  35.3 79.5 %collective-permute-start.2 = (bf16[8,512,1536]{2,1,0:T(8,128)(2,1)}, bf16[8,512,1536]{2,1,0:T(8,128)(2,1)}, u32[]{:S(2)}, u32[]{:S(2)}) collective-permute-start(bf16[8,512,1536]{2,1,0:T(8,128)(2,1)} %da.5), channel_id=1, source_target_pairs={{0,1},{1,0},{2,3},{3,2},{4,5},{5,4},{6,7},{7,6},{8,9},{9,8},{10,11... | collective-permute-start | bytes 37748744 | tf_op jit(solution)/shard_map/ppermute | solution.py:539
  58.7 659.8 %reduce-scatter.4.cloned.1.call-start = ((), (), s32[]{:S(2)}) async-start(), calls=%async_computation.5 | async-start | bytes 15728640 | tf_op jit(solution)/shard_map/reduce_scatter | solution.py:572
  195.1 527.4 %reduce-scatter.6.cloned.1.call-start = ((), (), s32[]{:S(2)}) async-start(), calls=%async_computation.7 | async-start | bytes 15728640 | tf_op jit(solution)/shard_map/reduce_scatter | solution.py:572
  291.7 599.9 %reduce-scatter.8.cloned.1.call-start = ((), (), s32[]{:S(2)}) async-start(), calls=%async_computation.8 | async-start | bytes 31457280 | tf_op jit(solution)/shard_map/reduce_scatter | solution.py:572
  334.9 72.6 %collective-permute-start.3 = (bf16[512,1536]{1,0:T(8,128)(2,1)}, bf16[512,1536]{1,0:T(8,128)(2,1)S(1)}, u32[]{:S(2)}, u32[]{:S(2)}) collective-permute-start(bf16[512,1536]{1,0:T(8,128)(2,1)} %get-tuple-element.30.refs_0_), channel_id=1, source_target_pairs={{0,2},{1,3},{2,4},{3,5},{4,6},{5,7},{6,0},{7,1},{8,10},{9,11},{10,... | collective-permute-start | bytes 4718600 | tf_op jit(solution)/shard_map/ppermute | solution.py:559
  338.7 71.2 %collective-permute-start.6 = (bf16[512,1536]{1,0:T(8,128)(2,1)}, bf16[512,1536]{1,0:T(8,128)(2,1)S(1)}, u32[]{:S(2)}, u32[]{:S(2)}) collective-permute-start(bf16[512,1536]{1,0:T(8,128)(2,1)} %get-tuple-element.31.refs_1_), channel_id=1, source_target_pairs={{0,6},{1,7},{2,0},{3,1},{4,2},{5,3},{6,4},{7,5},{8,14},{9,15},{10,... | collective-permute-start | bytes 4718600 | tf_op jit(solution)/shard_map/ppermute | solution.py:560
  338.7 138.6 %collective-permute-start.5 = (bf16[512,1536]{1,0:T(8,128)(2,1)}, bf16[512,1536]{1,0:T(8,128)(2,1)S(1)}, u32[]{:S(2)}, u32[]{:S(2)}) collective-permute-start(bf16[512,1536]{1,0:T(8,128)(2,1)} %get-tuple-element.30.refs_0_), channel_id=1, source_target_pairs={{0,6},{1,7},{2,0},{3,1},{4,2},{5,3},{6,4},{7,5},{8,14},{9,15},{10,... | collective-permute-start | bytes 4718600 | tf_op jit(solution)/shard_map/ppermute | solution.py:560
  338.7 138.6 %collective-permute-start.4 = (bf16[512,1536]{1,0:T(8,128)(2,1)}, bf16[512,1536]{1,0:T(8,128)(2,1)S(1)}, u32[]{:S(2)}, u32[]{:S(2)}) collective-permute-start(bf16[512,1536]{1,0:T(8,128)(2,1)} %get-tuple-element.31.refs_1_), channel_id=1, source_target_pairs={{0,2},{1,3},{2,4},{3,5},{4,6},{5,7},{6,0},{7,1},{8,10},{9,11},{10,... | collective-permute-start | bytes 4718600 | tf_op jit(solution)/shard_map/ppermute | solution.py:559
  407.5 111.8 %copy-start.4 = (bf16[512,1536]{1,0:T(8,128)(2,1)}, bf16[512,1536]{1,0:T(8,128)(2,1)S(1)}, u32[]{:S(2)}) copy-start(bf16[512,1536]{1,0:T(8,128)(2,1)S(1)} %collective-permute-done.3.refs_2_) | copy-start | bytes 4718596
  407.5 110.6 %collective-permute-start.7 = (bf16[512,1536]{1,0:T(8,128)(2,1)S(1)}, bf16[512,1536]{1,0:T(8,128)(2,1)S(1)}, u32[]{:S(2)}, u32[]{:S(2)}) collective-permute-start(bf16[512,1536]{1,0:T(8,128)(2,1)S(1)} %collective-permute-done.3.refs_2_), channel_id=1, source_target_pairs={{0,2},{1,3},{2,4},{3,5},{4,6},{5,7},{6,0},{7,1},{8,10},{9,11},{10,... | collective-permute-start | bytes 4718600 | tf_op jit(solution)/shard_map/ppermute | solution.py:561
  409.8 108.2 %copy-start.5 = (bf16[512,1536]{1,0:T(8,128)(2,1)}, bf16[512,1536]{1,0:T(8,128)(2,1)S(1)}, u32[]{:S(2)}) copy-start(bf16[512,1536]{1,0:T(8,128)(2,1)S(1)} %collective-permute-done.6.refs_5_) | copy-start | bytes 4718596
  409.8 109.4 %collective-permute-start.8 = (bf16[512,1536]{1,0:T(8,128)(2,1)S(1)}, bf16[512,1536]{1,0:T(8,128)(2,1)}, u32[]{:S(2)}, u32[]{:S(2)}) collective-permute-start(bf16[512,1536]{1,0:T(8,128)(2,1)S(1)} %collective-permute-done.6.refs_5_), channel_id=1, source_target_pairs={{0,6},{1,7},{2,0},{3,1},{4,2},{5,3},{6,4},{7,5},{8,14},{9,15},{10,... | collective-permute-start | bytes 4718600 | tf_op jit(solution)/shard_map/ppermute | solution.py:561
  477.3 40.8 %copy-start.6 = (bf16[512,1536]{1,0:T(8,128)(2,1)}, bf16[512,1536]{1,0:T(8,128)(2,1)S(1)}, u32[]{:S(2)}) copy-start(bf16[512,1536]{1,0:T(8,128)(2,1)S(1)} %collective-permute-done.5.refs_4_) | copy-start | bytes 4718596
  477.3 40.8 %copy-start.7 = (bf16[512,1536]{1,0:T(8,128)(2,1)}, bf16[512,1536]{1,0:T(8,128)(2,1)S(1)}, u32[]{:S(2)}) copy-start(bf16[512,1536]{1,0:T(8,128)(2,1)S(1)} %collective-permute-done.4.refs_3_) | copy-start | bytes 4718596
  674.6 1.4 copy-start.1
  676.0 1.9 copy-start.2
  676.0 2.8 copy-start.10
  678.8 6.3 copy-start.9
  678.8 3.1 copy-start.3
  (2 other events, 2.5 us)
Sparse Core Ops, SparseCore 0:
  9.2 22.0 all-gather.3
  34.6 64.4 all-gather.5
  100.6 62.1 all-gather.7
  195.2 111.0 reduce-scatter.3
  308.5 187.8 reduce-scatter.5
  674.8 216.7 reduce-scatter.7
